TPU v7x, 16 devices: a whole 2x2x2 slice. The times are simulated.
16 devices in a mesh: ez: 2 (over z), ey: 2 (over y), ex: 4 (over x, core).
Axes of the slice: x: 2, y: 2, z: 2, core: 2. Of those that a mesh axis runs over, the one named last changes fastest.
Arguments:
- tokens_in: bfloat16 [2, 4096, 1024], P(None, ('ez', 'ey', 'ex'))
- expert_ids: int32 [2, 2, 4096, 8], P(None, None, ('ez', 'ey', 'ex'))
- gate_vals: float32 [2, 2, 4096, 8], P(None, None, ('ez', 'ey', 'ex'))
- w_up1: bfloat16 [2, 32, 1024, 512], P(None, ('ez', 'ey', 'ex'))
- w_up3: bfloat16 [2, 32, 1024, 512], P(None, ('ez', 'ey', 'ex'))
- w_down: bfloat16 [2, 32, 512, 1024], P(None, ('ez', 'ey', 'ex'))
Outputs:
- output: bfloat16 [2, 4096, 1024], P(None, ('ez', 'ey', 'ex'))
All inputs are finite; a program needn't handle non-finite values.
Results may differ from a plain program's by a relative error of at most 0.0106397.
Values are sent between devices in bfloat16 or wider.
A program may use at most 1 GiB of HBM per device.

v0:
```python
import jax
import jax.numpy as jnp
from jax import lax
from jax.sharding import PartitionSpec as P

ROUTE_SCALE = 2.5
MESH_AXES = ("ez", "ey", "ex")


def capacity_of(tok_mb, top_k, experts):
    return 2 * ((tok_mb * top_k + experts - 1) // experts)


def slot_layout(ids_blk, gates_blk, first_slot, num_slots, experts, capacity):
    chosen = (ids_blk[..., None] == jnp.arange(experts)).astype(jnp.int32)
    per_expert = jnp.sum(chosen, axis=-2)
    token_rank = jnp.cumsum(per_expert, axis=-2) - per_expert
    slot_pos = jnp.sum(chosen * token_rank[..., None, :], axis=-1)
    flat_slot = ids_blk * capacity + slot_pos - first_slot
    slot_match = flat_slot[..., None] == jnp.arange(num_slots)
    dispatch = jnp.any(slot_match, axis=-2).astype(jnp.bfloat16)
    combine = jnp.sum(jnp.where(slot_match, gates_blk[..., None], 0.0), axis=-2)
    return dispatch, combine


def expert_ffn(expert_rows, mat_up1, mat_up3, mat_down):
    gate_in = jnp.einsum("eldi,lig->eldg", expert_rows, mat_up1, preferred_element_type=jnp.float32)
    lin_in = jnp.einsum("eldi,lig->eldg", expert_rows, mat_up3, preferred_element_type=jnp.float32)
    hidden = (jax.nn.silu(gate_in) * lin_in).astype(jnp.bfloat16)
    return jnp.einsum("dkcf,kfh->dkch", hidden, mat_down, preferred_element_type=jnp.float32).astype(jnp.bfloat16)


def solution(mesh):
    n_dev = mesh.shape["ez"] * mesh.shape["ey"] * mesh.shape["ex"]
    tok_spec = P(None, MESH_AXES, None)
    route_spec = P(None, None, MESH_AXES, None)
    weight_spec = P(None, MESH_AXES, None, None)

    def device_body(tokens_in, expert_ids, gate_vals, w_up1, w_up3, w_down):
        n_layers, n_micro, tok_mb, top_k = expert_ids.shape
        exp_dev = w_up1.shape[1]
        hidden_size = tokens_in.shape[-1]
        experts = exp_dev * n_dev
        capacity = capacity_of(tok_mb, top_k, experts)
        batches = [tokens_in[mb_idx] for mb_idx in range(n_micro)]
        for layer_idx in range(n_layers):
            for mb_idx in range(n_micro):
                tokens = batches[mb_idx]
                dispatch, combine = slot_layout(expert_ids[layer_idx, mb_idx], gate_vals[layer_idx, mb_idx], 0, experts * capacity, experts, capacity)
                send_buf = jnp.einsum("tn,th->nh", dispatch, tokens, preferred_element_type=jnp.float32).astype(jnp.bfloat16)
                send_buf = send_buf.reshape(n_dev, exp_dev, capacity, hidden_size)
                recv_buf = lax.all_to_all(send_buf, MESH_AXES, 0, 0, tiled=True)
                expert_out = expert_ffn(recv_buf, w_up1[layer_idx], w_up3[layer_idx], w_down[layer_idx])
                returned = lax.all_to_all(expert_out, MESH_AXES, 0, 0, tiled=True)
                moe_sum = jnp.dot(combine, returned.reshape(experts * capacity, hidden_size), preferred_element_type=jnp.float32)
                batches[mb_idx] = (tokens.astype(jnp.float32) + ROUTE_SCALE * moe_sum).astype(jnp.bfloat16)
        return jnp.stack(batches)

    return jax.shard_map(device_body, mesh=mesh, in_specs=(tok_spec, route_spec, route_spec, weight_spec, weight_spec, weight_spec), out_specs=tok_spec, check_vma=False)
```

profile of v0, /device:TPU:0, one launch (start us, length us, event | category | flops | bytes accessed | tf_op | source)
XLA Modules:
  0.0 929.2 jit_solution(207485099318160048)
XLA Ops:
  5.7 18.5 %fusion.3 = pred[256,4096]{1,0:T(8,128)(4,1)S(1)} fusion(s32[256,8]{1,0:T(8,128)S(1)} %copy.93), kind=kLoop, calls=%fused_computation.11 | loop fusion | flops 15728640 | bytes 1056768 | tf_op jit(solution)/shard_map/reduce_or | solution.py:21
  36.9 18.5 %fusion.1 = pred[256,4096]{1,0:T(8,128)(4,1)S(1)} fusion(s32[256,8]{1,0:T(8,128)S(1)} %copy.107), kind=kLoop, calls=%fused_computation.5 | loop fusion | flops 15728640 | bytes 1056768 | tf_op jit(solution)/shard_map/reduce_or | solution.py:21
  61.0 82.6 %all-to-all-done = bf16[16,2,128,1024]{3,2,1,0:T(8,128)(2,1)} async-done(((bf16[16,2,128,1024]{3,2,1,0:T(8,128)(2,1)}), bf16[16,2,128,1024]{3,2,1,0:T(8,128)(2,1)}, u32[]{:S(2)}, u32[]{:S(2)}) %all-to-all-start) | async-done | bytes 8388640 | tf_op jit(solution)/shard_map/all_to_all | solution.py:52
  147.8 11.7 %fusion.32 = f32[2,16,128,512]{3,2,1,0:T(8,128)} fusion(bf16[16,2,128,1024]{3,2,1,0:T(8,128)(2,1)} %all-to-all-done, bf16[2,2,1024,512]{3,2,1,0:T(8,128)(2,1)} %param.10), kind=kOutput, calls=%fused_computation.60 | convolution fusion | flops 4294967296 | bytes 18874368 | tf_op jit(solution)/shard_map/eldi,lig->eldg/dot_general | solution.py:28
  159.5 16.4 %convert_bitcast_fusion.3 = bf16[16,2,128,1024]{3,2,0,1:T(8,128)(2,1)} fusion(f32[2,16,128,512]{3,2,1,0:T(8,128)} %fusion.32, bf16[16,2,128,1024]{3,2,1,0:T(8,128)(2,1)} %all-to-all-done, bf16[2,2,512,1024]{3,2,1,0:T(8,128)(2,1)} %param.11, bf16[2,2,1024,512]{3,2,1,0:T(8,128)(2,1)} %param.9), kind=kOutput, calls=%fused_computation.43 | convolution fusion | flops 8606711808 | bytes 29360128 | tf_op jit(solution)/shard_map/dkcf,kfh->dkch/dot_general | solution.py:30
  184.1 70.7 %all-to-all-done.4 = bf16[16,2,128,1024]{3,2,1,0:T(8,128)(2,1)} async-done(((bf16[16,2,128,1024]{3,2,1,0:T(8,128)(2,1)}), bf16[16,2,128,1024]{3,2,1,0:T(8,128)(2,1)}, u32[]{:S(2)}, u32[]{:S(2)}) %all-to-all-start.4) | async-done | bytes 8388640 | tf_op jit(solution)/shard_map/all_to_all | solution.py:52
  259.0 11.7 %fusion.24 = f32[2,16,128,512]{3,2,1,0:T(8,128)} fusion(bf16[16,2,128,1024]{3,2,1,0:T(8,128)(2,1)} %all-to-all-done.4, bf16[2,2,1024,512]{3,2,1,0:T(8,128)(2,1)} %param.10), kind=kOutput, calls=%fused_computation.52 | convolution fusion | flops 4294967296 | bytes 18874368 | tf_op jit(solution)/shard_map/eldi,lig->eldg/dot_general | solution.py:28
  270.7 16.4 %convert_bitcast_fusion.1 = bf16[16,2,128,1024]{3,2,0,1:T(8,128)(2,1)} fusion(f32[2,16,128,512]{3,2,1,0:T(8,128)} %fusion.24, bf16[16,2,128,1024]{3,2,1,0:T(8,128)(2,1)} %all-to-all-done.4, bf16[2,2,512,1024]{3,2,1,0:T(8,128)(2,1)} %param.11, bf16[2,2,1024,512]{3,2,1,0:T(8,128)(2,1)} %param.9), kind=kOutput, calls=%fused_computation.41 | convolution fusion | flops 8606711808 | bytes 29360128 | tf_op jit(solution)/shard_map/dkcf,kfh->dkch/dot_general | solution.py:30
  295.2 70.7 %all-to-all-done.1 = bf16[16,2,128,1024]{3,2,1,0:T(8,128)(2,1)} async-done(((bf16[16,2,128,1024]{3,2,1,0:T(8,128)(2,1)}), bf16[16,2,128,1024]{3,2,1,0:T(8,128)(2,1)}, u32[]{:S(2)}, u32[]{:S(2)}) %all-to-all-start.1) | async-done | bytes 8388640 | tf_op jit(solution)/shard_map/all_to_all | solution.py:54
  370.6 18.5 %fusion.2 = pred[256,4096]{1,0:T(8,128)(4,1)S(1)} fusion(s32[256,8]{1,0:T(8,128)S(1)} %copy.100), kind=kLoop, calls=%fused_computation.8 | loop fusion | flops 15728640 | bytes 1056768 | tf_op jit(solution)/shard_map/reduce_or | solution.py:21
  389.1 17.0 %select_reduce_fusion.3 = bf16[256,4096]{1,0:T(8,128)(2,1)S(1)} fusion(f32[256,8]{1,0:T(8,128)S(1)} %copy.94, s32[256,8]{1,0:T(8,128)S(1)} %copy.93), kind=kLoop, calls=%fused_computation.9 | loop fusion | flops 24117248 | bytes 2113536 | tf_op jit(solution)/shard_map/reduce_sum | solution.py:22
  417.5 59.7 %all-to-all-done.5 = bf16[16,2,128,1024]{3,2,1,0:T(8,128)(2,1)} async-done(((bf16[16,2,128,1024]{3,2,1,0:T(8,128)(2,1)}), bf16[16,2,128,1024]{3,2,1,0:T(8,128)(2,1)}, u32[]{:S(2)}, u32[]{:S(2)}) %all-to-all-start.5) | async-done | bytes 8388640 | tf_op jit(solution)/shard_map/all_to_all | solution.py:54
  481.7 18.5 %fusion = pred[256,4096]{1,0:T(8,128)(4,1)S(1)} fusion(s32[256,8]{1,0:T(8,128)S(1)} %copy.114), kind=kLoop, calls=%fused_computation.2 | loop fusion | flops 15728640 | bytes 1056768 | tf_op jit(solution)/shard_map/reduce_or | solution.py:21
  500.2 17.0 %select_reduce_fusion.1 = bf16[256,4096]{1,0:T(8,128)(2,1)S(1)} fusion(f32[256,8]{1,0:T(8,128)S(1)} %copy.108, s32[256,8]{1,0:T(8,128)S(1)} %copy.107), kind=kLoop, calls=%fused_computation.3 | loop fusion | flops 24117248 | bytes 2113536 | tf_op jit(solution)/shard_map/reduce_sum | solution.py:22
  528.6 59.7 %all-to-all-done.2 = bf16[16,2,128,1024]{3,2,1,0:T(8,128)(2,1)} async-done(((bf16[16,2,128,1024]{3,2,1,0:T(8,128)(2,1)}), bf16[16,2,128,1024]{3,2,1,0:T(8,128)(2,1)}, u32[]{:S(2)}, u32[]{:S(2)}) %all-to-all-start.2) | async-done | bytes 8388640 | tf_op jit(solution)/shard_map/all_to_all | solution.py:52
  592.6 11.7 %fusion.28 = f32[2,16,128,512]{3,2,1,0:T(8,128)} fusion(bf16[16,2,128,1024]{3,2,1,0:T(8,128)(2,1)} %all-to-all-done.2, bf16[2,2,1024,512]{3,2,1,0:T(8,128)(2,1)} %param.10), kind=kOutput, calls=%fused_computation.56 | convolution fusion | flops 4294967296 | bytes 18874368 | tf_op jit(solution)/shard_map/eldi,lig->eldg/dot_general | solution.py:28
  604.3 16.4 %convert_bitcast_fusion.2 = bf16[16,2,128,1024]{3,2,0,1:T(8,128)(2,1)} fusion(f32[2,16,128,512]{3,2,1,0:T(8,128)} %fusion.28, bf16[16,2,128,1024]{3,2,1,0:T(8,128)(2,1)} %all-to-all-done.2, bf16[2,2,512,1024]{3,2,1,0:T(8,128)(2,1)} %param.11, bf16[2,2,1024,512]{3,2,1,0:T(8,128)(2,1)} %param.9), kind=kOutput, calls=%fused_computation.42 | convolution fusion | flops 8606711808 | bytes 29360128 | tf_op jit(solution)/shard_map/dkcf,kfh->dkch/dot_general | solution.py:30
  628.8 70.7 %all-to-all-done.6 = bf16[16,2,128,1024]{3,2,1,0:T(8,128)(2,1)} async-done(((bf16[16,2,128,1024]{3,2,1,0:T(8,128)(2,1)}), bf16[16,2,128,1024]{3,2,1,0:T(8,128)(2,1)}, u32[]{:S(2)}, u32[]{:S(2)}) %all-to-all-start.6) | async-done | bytes 8388640 | tf_op jit(solution)/shard_map/all_to_all | solution.py:52
  703.8 11.7 %fusion.20 = f32[2,16,128,512]{3,2,1,0:T(8,128)} fusion(bf16[16,2,128,1024]{3,2,1,0:T(8,128)(2,1)} %all-to-all-done.6, bf16[2,2,1024,512]{3,2,1,0:T(8,128)(2,1)} %param.10), kind=kOutput, calls=%fused_computation.48 | convolution fusion | flops 4294967296 | bytes 18874368 | tf_op jit(solution)/shard_map/eldi,lig->eldg/dot_general | solution.py:28
  715.5 16.4 %convert_bitcast_fusion = bf16[16,2,128,1024]{3,2,0,1:T(8,128)(2,1)} fusion(f32[2,16,128,512]{3,2,1,0:T(8,128)} %fusion.20, bf16[16,2,128,1024]{3,2,1,0:T(8,128)(2,1)} %all-to-all-done.6, bf16[2,2,512,1024]{3,2,1,0:T(8,128)(2,1)} %param.11, bf16[2,2,1024,512]{3,2,1,0:T(8,128)(2,1)} %param.9), kind=kOutput, calls=%fused_computation.40 | convolution fusion | flops 8606711808 | bytes 29360128 | tf_op jit(solution)/shard_map/dkcf,kfh->dkch/dot_general | solution.py:30
  740.0 70.7 %all-to-all-done.3 = bf16[16,2,128,1024]{3,2,1,0:T(8,128)(2,1)} async-done(((bf16[16,2,128,1024]{3,2,1,0:T(8,128)(2,1)}), bf16[16,2,128,1024]{3,2,1,0:T(8,128)(2,1)}, u32[]{:S(2)}, u32[]{:S(2)}) %all-to-all-start.3) | async-done | bytes 8388640 | tf_op jit(solution)/shard_map/all_to_all | solution.py:54
  815.2 17.0 %select_reduce_fusion.2 = bf16[256,4096]{1,0:T(8,128)(2,1)S(1)} fusion(f32[256,8]{1,0:T(8,128)S(1)} %copy.101, s32[256,8]{1,0:T(8,128)S(1)} %copy.100), kind=kLoop, calls=%fused_computation.6 | loop fusion | flops 24117248 | bytes 2113536 | tf_op jit(solution)/shard_map/reduce_sum | solution.py:22
  832.2 17.0 %select_reduce_fusion = bf16[256,4096]{1,0:T(8,128)(2,1)S(1)} fusion(f32[256,8]{1,0:T(8,128)S(1)} %copy.115, s32[256,8]{1,0:T(8,128)S(1)} %copy.114), kind=kLoop, calls=%fused_computation | loop fusion | flops 24117248 | bytes 2113536 | tf_op jit(solution)/shard_map/reduce_sum | solution.py:22
  855.0 66.9 %all-to-all-done.7 = bf16[16,2,128,1024]{3,2,1,0:T(8,128)(2,1)} async-done(((bf16[16,2,128,1024]{3,2,1,0:T(8,128)(2,1)}), bf16[16,2,128,1024]{3,2,1,0:T(8,128)(2,1)}, u32[]{:S(2)}, u32[]{:S(2)}) %all-to-all-start.7) | async-done | bytes 8388640 | tf_op jit(solution)/shard_map/all_to_all | solution.py:54
  (72 shorter events, 122.6 us)
Async XLA Ops:
  30.8 24.6 %copy-start.1 = (bf16[2,256,1024]{2,1,0:T(8,128)(2,1)S(1)}, bf16[2,256,1024]{2,1,0:T(8,128)(2,1)}, u32[]{:S(2)}) copy-start(bf16[2,256,1024]{2,1,0:T(8,128)(2,1)} %param.6) | copy-start | bytes 3145732
  30.8 112.8 %all-to-all-start = ((bf16[16,2,128,1024]{3,2,1,0:T(8,128)(2,1)}), bf16[16,2,128,1024]{3,2,1,0:T(8,128)(2,1)}, u32[]{:S(2)}, u32[]{:S(2)}) async-start(bf16[16,2,128,1024]{3,2,1,0:T(8,128)(2,1)} %bitcast.265), calls=%async_computation | async-start | bytes 16777216 | tf_op jit(solution)/shard_map/all_to_all | solution.py:52
  143.6 111.1 %all-to-all-start.4 = ((bf16[16,2,128,1024]{3,2,1,0:T(8,128)(2,1)}), bf16[16,2,128,1024]{3,2,1,0:T(8,128)(2,1)}, u32[]{:S(2)}, u32[]{:S(2)}) async-start(bf16[16,2,128,1024]{3,2,1,0:T(8,128)(2,1)} %bitcast.263), calls=%async_computation.4 | async-start | bytes 16777216 | tf_op jit(solution)/shard_map/all_to_all | solution.py:52
  254.7 111.1 %all-to-all-start.1 = ((bf16[16,2,128,1024]{3,2,1,0:T(8,128)(2,1)}), bf16[16,2,128,1024]{3,2,1,0:T(8,128)(2,1)}, u32[]{:S(2)}, u32[]{:S(2)}) async-start(bf16[16,2,128,1024]{3,2,1,0:T(8,128)(2,1)} %copy.97), calls=%async_computation.1 | async-start | bytes 16777216 | tf_op jit(solution)/shard_map/all_to_all | solution.py:54
  295.2 75.1 %copy-start = (f32[2,2,256,8]{2,3,1,0:T(8,128)S(1)}, f32[2,2,256,8]{2,3,1,0:T(8,128)}, u32[]{:S(2)}) copy-start(f32[2,2,256,8]{2,3,1,0:T(8,128)} %param.8) | copy-start | bytes 98308
  365.9 111.3 %all-to-all-start.5 = ((bf16[16,2,128,1024]{3,2,1,0:T(8,128)(2,1)}), bf16[16,2,128,1024]{3,2,1,0:T(8,128)(2,1)}, u32[]{:S(2)}, u32[]{:S(2)}) async-start(bf16[16,2,128,1024]{3,2,1,0:T(8,128)(2,1)} %copy.111), calls=%async_computation.5 | async-start | bytes 16777216 | tf_op jit(solution)/shard_map/all_to_all | solution.py:54
  411.9 65.3 %copy-start.2 = (bf16[256,1024]{1,0:T(8,128)(2,1)}, bf16[256,1024]{1,0:T(8,128)(2,1)S(1)}, u32[]{:S(2)}) copy-start(bf16[256,1024]{1,0:T(8,128)(2,1)S(1)} %fusion.99) | copy-start | bytes 1572868
  477.2 111.1 %all-to-all-start.2 = ((bf16[16,2,128,1024]{3,2,1,0:T(8,128)(2,1)}), bf16[16,2,128,1024]{3,2,1,0:T(8,128)(2,1)}, u32[]{:S(2)}, u32[]{:S(2)}) async-start(bf16[16,2,128,1024]{3,2,1,0:T(8,128)(2,1)} %bitcast.262), calls=%async_computation.2 | async-start | bytes 16777216 | tf_op jit(solution)/shard_map/all_to_all | solution.py:52
  523.0 65.3 %copy-start.4 = (bf16[256,1024]{1,0:T(8,128)(2,1)}, bf16[256,1024]{1,0:T(8,128)(2,1)S(1)}, u32[]{:S(2)}) copy-start(bf16[256,1024]{1,0:T(8,128)(2,1)S(1)} %fusion.97) | copy-start | bytes 1572868
  588.3 111.1 %all-to-all-start.6 = ((bf16[16,2,128,1024]{3,2,1,0:T(8,128)(2,1)}), bf16[16,2,128,1024]{3,2,1,0:T(8,128)(2,1)}, u32[]{:S(2)}, u32[]{:S(2)}) async-start(bf16[16,2,128,1024]{3,2,1,0:T(8,128)(2,1)} %bitcast.264), calls=%async_computation.6 | async-start | bytes 16777216 | tf_op jit(solution)/shard_map/all_to_all | solution.py:52
  699.5 111.2 %all-to-all-start.3 = ((bf16[16,2,128,1024]{3,2,1,0:T(8,128)(2,1)}), bf16[16,2,128,1024]{3,2,1,0:T(8,128)(2,1)}, u32[]{:S(2)}, u32[]{:S(2)}) async-start(bf16[16,2,128,1024]{3,2,1,0:T(8,128)(2,1)} %copy.104), calls=%async_computation.3 | async-start | bytes 16777216 | tf_op jit(solution)/shard_map/all_to_all | solution.py:54
  740.0 109.2 %copy-start.3 = (bf16[256,1024]{1,0:T(8,128)(2,1)S(1)}, bf16[256,1024]{1,0:T(8,128)(2,1)}, u32[]{:S(2)}) copy-start(bf16[256,1024]{1,0:T(8,128)(2,1)} %copy-done.2) | copy-start | bytes 1572868
  810.7 111.2 %all-to-all-start.7 = ((bf16[16,2,128,1024]{3,2,1,0:T(8,128)(2,1)}), bf16[16,2,128,1024]{3,2,1,0:T(8,128)(2,1)}, u32[]{:S(2)}, u32[]{:S(2)}) async-start(bf16[16,2,128,1024]{3,2,1,0:T(8,128)(2,1)} %copy.118), calls=%async_computation.7 | async-start | bytes 16777216 | tf_op jit(solution)/shard_map/all_to_all | solution.py:54
where the time goes:
time: 935 us; the launch traced here: 929 us
  waiting for transfers between devices  552 us (59%)
  matrix products  159 us (17%)
  other arithmetic  147 us (16%)
  starting transfers between devices  35.8 us (4%)
  local copies, waits for them, and re-layouts  35.3 us (4%)
    all_to_all x4, waiting for transfers between devices, device_body(): recv_buf = lax.all_to_all(send_buf, MESH_AXES, 0, 0, tiled=True)  284 us
    all_to_all x4, waiting for transfers between devices, device_body(): returned = lax.all_to_all(expert_out, MESH_AXES, 0, 0, tiled=True)  268 us
    reduce_or x4, other arithmetic, slot_layout(): dispatch = jnp.any(slot_match, axis=-2).astype(jnp.bfloat16)  74.1 us
    reduce_sum x4, other arithmetic, slot_layout(): combine = jnp.sum(jnp.where(slot_match, gates_blk[..., None], 0.0), axis=-2)  67.9 us
    dot_general x4, matrix products, expert_ffn(): jnp.einsum('dkcf,kfh->dkch', hidden, mat_down, preferred_element_type=jnp...  65.4 us
    dot_general x4, matrix products, expert_ffn(): jnp.einsum('eldi,lig->eldg', expert_rows, mat_up3, preferred_element_type...  46.8 us
    convert_element_type x4, local copies, waits for them, and re-layouts, expert_ffn(): jnp.einsum('dkcf,kfh->dkch', hidden, mat_down, preferred_element_type=jnp...  32.8 us
    dot_general x4, matrix products, device_body(): jnp.einsum('tn,th->nh', dispatch, tokens, preferred_element_type=jnp.floa...  23.5 us
  transfers between devices with their start and end apart: 8, of which 8 were waited for; matrix products, arithmetic and copies ran while one was open for 33% of the time, Pallas kernels for 0%

commit v1 on v0

v1 whole, which is shorter than its diff:
```python
import jax
import jax.numpy as jnp
from jax import lax
from jax.sharding import PartitionSpec as P

ROUTE_SCALE = 2.5
MESH_AXES = ("ez", "ey", "ex")


def solution(mesh):
    n_dev = mesh.shape["ez"] * mesh.shape["ey"] * mesh.shape["ex"]
    tok_spec = P(None, MESH_AXES, None)
    route_spec = P(None, None, MESH_AXES, None)
    weight_spec = P(None, MESH_AXES, None, None)

    def device_body(tokens_in, expert_ids, gate_vals, w_up1, w_up3, w_down):
        n_layers, n_micro, tok_mb, top_k = expert_ids.shape
        exp_dev = w_up1.shape[1]
        experts = exp_dev * n_dev
        hot = expert_ids[..., None] == jnp.arange(experts)
        table = jnp.sum(jnp.where(hot, gate_vals[..., None], 0.0), axis=-2)
        table = table.reshape(n_layers, n_micro, tok_mb, n_dev, exp_dev)
        table = lax.all_to_all(table, MESH_AXES, 3, 2, tiled=True)
        table = table.reshape(n_layers, n_micro, n_dev * tok_mb, exp_dev)
        batches = [tokens_in[mb_idx] for mb_idx in range(n_micro)]
        for layer_idx in range(n_layers):
            for mb_idx in range(n_micro):
                tokens = batches[mb_idx]
                everyone = lax.all_gather(tokens, MESH_AXES, axis=0, tiled=True)
                total = jnp.zeros(everyone.shape, jnp.float32)
                for e in range(exp_dev):
                    a = jnp.dot(everyone, w_up1[layer_idx, e], preferred_element_type=jnp.float32)
                    b = jnp.dot(everyone, w_up3[layer_idx, e], preferred_element_type=jnp.float32)
                    h = (jax.nn.silu(a) * b).astype(jnp.bfloat16)
                    o = jnp.dot(h, w_down[layer_idx, e], preferred_element_type=jnp.float32).astype(jnp.bfloat16)
                    g = table[layer_idx, mb_idx, :, e][:, None]
                    total = total + jnp.where(g > 0.0, g * o.astype(jnp.float32), 0.0)
                moe_sum = lax.psum_scatter(total, MESH_AXES, scatter_dimension=0, tiled=True)
                batches[mb_idx] = (tokens.astype(jnp.float32) + ROUTE_SCALE * moe_sum).astype(jnp.bfloat16)
        return jnp.stack(batches)

    return jax.shard_map(device_body, mesh=mesh, in_specs=(tok_spec, route_spec, route_spec, weight_spec, weight_spec, weight_spec), out_specs=tok_spec, check_vma=False)
```

time: 935 us -> 953 us (1.019)
  other arithmetic: 147 us -> 7.68 us
  waiting for transfers between devices: 552 us -> 680 us
  matrix products: 159 us -> 227 us
  starting transfers between devices: 35.8 us -> 0.67 us
  local copies, waits for them, and re-layouts: 35.3 us -> 3.75 us
  between operations: 0.87 us -> 14 us
  blocking collectives: 0 us -> 11.4 us
    reduce_scatter x0 -> x4, waiting for transfers between devices: none -> 594 us  [device_body(): lax.psum_scatter(total, MESH_AXES, scatter_dimension=0, tiled=True)]
    all_to_all x8 -> x0, waiting for transfers between devices: 552 us -> none  [the longest x4 284 us: device_body(): recv_buf = lax.all_to_all(send_buf, MESH_AXES, 0, 0, tiled=True)]
    all_gather x0 -> x4, waiting for transfers between devices: none -> 84.3 us  [device_body(): everyone = lax.all_gather(tokens, MESH_AXES, axis=0, tiled=True)]
    reduce_or x4 -> x0, other arithmetic: 74.1 us -> none  [slot_layout(): dispatch = jnp.any(slot_match, axis=-2).astype(jnp.bfloat16)]
    dot_general x16, matrix products: 159 us -> 227 us  [the longest x8 148 us: device_body(): jnp.dot(h, w_down[layer_idx, e], preferred_element_type=jnp.float32)]
    reduce_sum x10 -> x1, other arithmetic: 68.2 us -> 0.94 us  [device_body(): table = jnp.sum(jnp.where(hot, gate_vals[..., None], 0.0), axis=-2)]
    all_to_all x8 -> x0, starting transfers between devices: 35.8 us -> none  [the longest x4 18.5 us: device_body(): recv_buf = lax.all_to_all(send_buf, MESH_AXES, 0, 0, tiled=True)]
    convert_element_type x4 -> x0, local copies, waits for them, and re-layouts: 32.8 us -> none  [expert_ffn(): jnp.einsum('dkcf,kfh->dkch', hidden, mat_down, preferred_element_type=jnp...]
  transfers between devices with their start and end apart: 8 -> 8, of which waited for: 8 -> 6; matrix products, arithmetic and copies ran while one was open for 33% -> 24% of each run, Pallas kernels for 0% -> 0%
where the time goes in v1:
time: 953 us; the launch traced here: 944 us
  waiting for transfers between devices  680 us (71%)
  matrix products  227 us (24%)
  between operations  14 us (1%)
  blocking collectives  11.4 us (1%)
    reduce_scatter x4, waiting for transfers between devices, device_body(): lax.psum_scatter(total, MESH_AXES, scatter_dimension=0, tiled=True)  594 us
    dot_general x8, matrix products, device_body(): jnp.dot(h, w_down[layer_idx, e], preferred_element_type=jnp.float32)  148 us
    all_gather x4, waiting for transfers between devices, device_body(): everyone = lax.all_gather(tokens, MESH_AXES, axis=0, tiled=True)  84.3 us
    dot_general x8, matrix products, device_body(): jnp.dot(everyone, w_up1[layer_idx, e], preferred_element_type=jnp.float32)  79 us
  transfers between devices with their start and end apart: 8, of which 6 were waited for; matrix products, arithmetic and copies ran while one was open for 24% of the time, Pallas kernels for 0%

profile of v1, /device:TPU:0, one launch (start us, length us, event | category | flops | bytes accessed | tf_op | source)
XLA Modules:
  0.0 944.3 jit_solution(15773214516711695688)
XLA Ops:
  10.7 11.4 %all_to_all.15 = f32[2,2,256,16,2]{2,1,4,0,3:T(2,128)S(1)} all-to-all(f32[2,2,256,16,2]{2,1,4,0,3:T(2,128)S(1)} %copy.17), channel_id=1, replica_groups=mesh['ez'=2,'ey'=2,'ex'=4] {'ez','ey','ex'}, dimensions={3} | all-to-all | bytes 262144 | tf_op jit(solution)/shard_map/all_to_all | solution.py:23
  23.0 38.1 %all-gather.13.cloned.1.call-done = bf16[1,4096,1024]{2,1,0:T(8,128)(2,1)} async-done(((bf16[1,256,1024]{2,1,0:T(8,128)(2,1)}), bf16[1,4096,1024]{2,1,0:T(8,128)(2,1)}) %all-gather.13.cloned.1.call-update) | async-done | bytes 8388624 | tf_op jit(solution)/shard_map/all_gather | solution.py:29
  61.1 11.6 %fusion.6 = f32[4096,512]{1,0:T(8,128)} fusion(bf16[1,4096,1024]{2,1,0:T(8,128)(2,1)} %all-gather.13.cloned.1.call-done, bf16[2,2,1024,512]{3,2,1,0:T(8,128)(2,1)} %param.9), kind=kOutput, calls=%fused_computation.10 | convolution fusion | flops 4294967296 | bytes 17825792 | tf_op jit(solution)/shard_map/dot_general | solution.py:32
  72.6 8.1 fusion.2
  80.7 16.0 %fusion.28 = bf16[4096,1024]{1,0:T(8,128)(2,1)} fusion(f32[4096,512]{1,0:T(8,128)} %fusion.6, bf16[1,4096,1024]{2,1,0:T(8,128)(2,1)} %all-gather.13.cloned.1.call-done, bf16[2,2,512,1024]{3,2,1,0:T(8,128)(2,1)} %param.11, bf16[2,2,1024,512]{3,2,1,0:T(8,128)(2,1)} %param.10), kind=kOutput, calls=%fused_computation.29 | convolution fusion | flops 8602517504 | bytes 27262976 | tf_op jit(solution)/shard_map/dot_general | solution.py:35
  96.7 21.1 %select_add_fusion.1 = f32[4096,1024]{1,0:T(8,128)} fusion(f32[4096]{0:T(1024)S(1)} %bitcast.151, bf16[4096,1024]{1,0:T(8,128)(2,1)} %fusion.28, f32[4096]{0:T(1024)S(1)} %bitcast.153, pred[4096]{0:T(1024)(128)(4,1)S(1)} %get-tuple-element.19, pred[4096]{0:T(1024)(128)(4,1)S(1)} %get-tuple-element.20, f32[4096,512]{1,0:T(8,128)} %fusion.2, ...), kind=kOutput, calls=%fused_computation.1 | convolution fusion | flops 8636071936 | bytes 44081152 | tf_op jit(solution)/shard_map/dot_general | solution.py:35
  117.9 11.6 %fusion.14 = f32[4096,512]{1,0:T(8,128)} fusion(bf16[1,4096,1024]{2,1,0:T(8,128)(2,1)} %all-gather.11.cloned.1.call-done, bf16[2,2,1024,512]{3,2,1,0:T(8,128)(2,1)} %param.9), kind=kOutput, calls=%fused_computation.18 | convolution fusion | flops 4294967296 | bytes 17825792 | tf_op jit(solution)/shard_map/dot_general | solution.py:32
  129.5 8.5 fusion.10
  138.0 16.0 %fusion.25 = bf16[4096,1024]{1,0:T(8,128)(2,1)} fusion(f32[4096,512]{1,0:T(8,128)} %fusion.14, bf16[1,4096,1024]{2,1,0:T(8,128)(2,1)} %all-gather.11.cloned.1.call-done, bf16[2,2,512,1024]{3,2,1,0:T(8,128)(2,1)} %param.11, bf16[2,2,1024,512]{3,2,1,0:T(8,128)(2,1)} %param.10), kind=kOutput, calls=%fused_computation.28 | convolution fusion | flops 8602517504 | bytes 27262976 | tf_op jit(solution)/shard_map/dot_general | solution.py:35
  154.0 20.9 %select_add_fusion.3 = f32[4096,1024]{1,0:T(8,128)} fusion(f32[4096]{0:T(1024)S(1)} %bitcast.147, bf16[4096,1024]{1,0:T(8,128)(2,1)} %fusion.25, f32[4096]{0:T(1024)S(1)} %bitcast.149, pred[4096]{0:T(1024)(128)(4,1)S(1)} %get-tuple-element.17, pred[4096]{0:T(1024)(128)(4,1)S(1)} %get-tuple-element.18, f32[4096,512]{1,0:T(8,128)} %fusion.10, ...), kind=kOutput, calls=%fused_computation.3 | convolution fusion | flops 8636071936 | bytes 44081152 | tf_op jit(solution)/shard_map/dot_general | solution.py:35
  175.0 120.3 %reduce-scatter.9.cloned.1.call-done = f32[256,1024]{1,0:T(8,128)} async-done(((f32[4096,1024]{1,0:T(8,128)}), f32[256,1024]{1,0:T(8,128)}) %reduce-scatter.9.cloned.1.call-update) | async-done | bytes 1048592 | tf_op jit(solution)/shard_map/reduce_scatter | solution.py:38
  295.3 177.6 %reduce-scatter.5.cloned.1.call-done = f32[256,1024]{1,0:T(8,128)} async-done(((f32[4096,1024]{1,0:T(8,128)}), f32[256,1024]{1,0:T(8,128)}) %reduce-scatter.5.cloned.1.call-update) | async-done | bytes 1048592 | tf_op jit(solution)/shard_map/reduce_scatter | solution.py:38
  472.9 2.9 fusion.41
  476.7 46.2 %all-gather.7.cloned.1.call-done = bf16[4096,1024]{1,0:T(8,128)(2,1)} async-done(((bf16[256,1024]{1,0:T(8,128)(2,1)}), bf16[4096,1024]{1,0:T(8,128)(2,1)}) %all-gather.7.cloned.1.call-update) | async-done | bytes 8388624 | tf_op jit(solution)/shard_map/all_gather | solution.py:29
  522.9 11.6 %fusion.60 = f32[4096,512]{1,0:T(8,128)} fusion(bf16[4096,1024]{1,0:T(8,128)(2,1)} %all-gather.7.cloned.1.call-done, bf16[2,2,1024,512]{3,2,1,0:T(8,128)(2,1)} %param.9), kind=kOutput, calls=%fused_computation.55 | convolution fusion | flops 4294967296 | bytes 17825792 | tf_op jit(solution)/shard_map/dot_general | solution.py:32
  534.4 8.1 fusion.50
  542.5 16.0 %fusion.30 = bf16[4096,1024]{1,0:T(8,128)(2,1)} fusion(f32[4096,512]{1,0:T(8,128)} %fusion.60, bf16[4096,1024]{1,0:T(8,128)(2,1)} %all-gather.7.cloned.1.call-done, bf16[2,2,512,1024]{3,2,1,0:T(8,128)(2,1)} %param.11, bf16[2,2,1024,512]{3,2,1,0:T(8,128)(2,1)} %param.10), kind=kOutput, calls=%fused_computation.30 | convolution fusion | flops 8602517504 | bytes 27262976 | tf_op jit(solution)/shard_map/dot_general | solution.py:35
  558.5 20.9 %select_add_fusion.2 = f32[4096,1024]{1,0:T(8,128)} fusion(f32[4096]{0:T(1024)S(1)} %bitcast.145, bf16[4096,1024]{1,0:T(8,128)(2,1)} %fusion.30, f32[4096]{0:T(1024)S(1)} %bitcast.143, pred[4096]{0:T(1024)(128)(4,1)S(1)} %get-tuple-element.23, pred[4096]{0:T(1024)(128)(4,1)S(1)} %get-tuple-element.24, f32[4096,512]{1,0:T(8,128)} %fusion.50, ...), kind=kOutput, calls=%fused_computation.2 | convolution fusion | flops 8636071936 | bytes 44081152 | tf_op jit(solution)/shard_map/dot_general | solution.py:35
  580.2 11.6 %fusion.58 = f32[4096,512]{1,0:T(8,128)} fusion(bf16[4096,1024]{1,0:T(8,128)(2,1)} %all-gather.9.cloned.1.call-done, bf16[2,2,1024,512]{3,2,1,0:T(8,128)(2,1)} %param.9), kind=kOutput, calls=%fused_computation.53 | convolution fusion | flops 4294967296 | bytes 17825792 | tf_op jit(solution)/shard_map/dot_general | solution.py:32
  591.8 8.1 fusion.48
  599.9 16.0 %fusion.31 = bf16[4096,1024]{1,0:T(8,128)(2,1)} fusion(f32[4096,512]{1,0:T(8,128)} %fusion.58, bf16[4096,1024]{1,0:T(8,128)(2,1)} %all-gather.9.cloned.1.call-done, bf16[2,2,512,1024]{3,2,1,0:T(8,128)(2,1)} %param.11, bf16[2,2,1024,512]{3,2,1,0:T(8,128)(2,1)} %param.10), kind=kOutput, calls=%fused_computation.31 | convolution fusion | flops 8602517504 | bytes 27262976 | tf_op jit(solution)/shard_map/dot_general | solution.py:35
  615.9 20.9 %select_add_fusion = f32[4096,1024]{1,0:T(8,128)} fusion(f32[4096]{0:T(1024)S(1)} %bitcast.139, bf16[4096,1024]{1,0:T(8,128)(2,1)} %fusion.31, f32[4096]{0:T(1024)S(1)} %bitcast.141, pred[4096]{0:T(1024)(128)(4,1)S(1)} %get-tuple-element.21, pred[4096]{0:T(1024)(128)(4,1)S(1)} %get-tuple-element.22, f32[4096,512]{1,0:T(8,128)} %fusion.48, ...), kind=kOutput, calls=%fused_computation | convolution fusion | flops 8636071936 | bytes 44081152 | tf_op jit(solution)/shard_map/dot_general | solution.py:35
  636.8 120.0 %reduce-scatter.7.cloned.1.call-done = f32[256,1024]{1,0:T(8,128)} async-done(((f32[4096,1024]{1,0:T(8,128)}), f32[256,1024]{1,0:T(8,128)}) %reduce-scatter.7.cloned.1.call-update) | async-done | bytes 1048592 | tf_op jit(solution)/shard_map/reduce_scatter | solution.py:38
  758.3 176.4 %reduce-scatter.11.cloned.1.call-done = f32[256,1024]{1,0:T(8,128)} async-done(((f32[4096,1024]{1,0:T(8,128)}), f32[256,1024]{1,0:T(8,128)}) %reduce-scatter.11.cloned.1.call-update) | async-done | bytes 1048592 | tf_op jit(solution)/shard_map/reduce_scatter | solution.py:38
  (54 shorter events, 10.6 us)
Async XLA Ops:
  6.5 54.5 %all-gather.13.cloned.1.call-start = ((), (), s32[]{:S(2)}) async-start(), calls=%async_computation.12 | async-start | bytes 8912896 | tf_op jit(solution)/shard_map/all_gather | solution.py:29
  8.9 109.1 %all-gather.11.cloned.1.call-start = ((), (), s32[]{:S(2)}) async-start(), calls=%async_computation.11 | async-start | bytes 8912896 | tf_op jit(solution)/shard_map/all_gather | solution.py:29
  9.6 285.7 %reduce-scatter.9.cloned.1.call-start = ((), (), s32[]{:S(2)}) async-start(), calls=%async_computation.8 | async-start | bytes 17825792 | tf_op jit(solution)/shard_map/reduce_scatter | solution.py:38
  61.1 11.6 %copy-start.8 = (bf16[1,4096,1024]{2,1,0:T(8,128)(2,1)S(1)}, bf16[1,4096,1024]{2,1,0:T(8,128)(2,1)}, u32[]{:S(2)}) copy-start(bf16[1,4096,1024]{2,1,0:T(8,128)(2,1)} %all-gather.13.cloned.1.call-done) | copy-start | bytes 25165828
  117.8 355.1 %reduce-scatter.5.cloned.1.call-start = ((), (), s32[]{:S(2)}) async-start(), calls=%async_computation.5 | async-start | bytes 17825792 | tf_op jit(solution)/shard_map/reduce_scatter | solution.py:38
  117.9 11.6 %copy-start.7 = (bf16[1,4096,1024]{2,1,0:T(8,128)(2,1)S(1)}, bf16[1,4096,1024]{2,1,0:T(8,128)(2,1)}, u32[]{:S(2)}) copy-start(bf16[1,4096,1024]{2,1,0:T(8,128)(2,1)} %all-gather.11.cloned.1.call-done) | copy-start | bytes 25165828
  174.9 298.0 %copy-start.2 = (bf16[2,256,1024]{2,1,0:T(8,128)(2,1)S(1)}, bf16[2,256,1024]{2,1,0:T(8,128)(2,1)}, u32[]{:S(2)}) copy-start(bf16[2,256,1024]{2,1,0:T(8,128)(2,1)} %param.6) | copy-start | bytes 3145732
  174.9 301.7 %copy-start.5 = (f32[1,1,4096,1]{2,3,1,0:T(1,128)S(1)}, f32[1,1,4096,1]{2,3,1,0:T(1,128)}, u32[]{:S(2)}) copy-start(f32[1,1,4096,1]{2,3,1,0:T(1,128)} %get-tuple-element.9) | copy-start | bytes 49156
  174.9 301.7 %copy-start.6 = (f32[1,1,4096,1]{2,3,1,0:T(1,128)S(1)}, f32[1,1,4096,1]{2,3,1,0:T(1,128)}, u32[]{:S(2)}) copy-start(f32[1,1,4096,1]{2,3,1,0:T(1,128)} %get-tuple-element.14) | copy-start | bytes 49156
  175.0 347.9 %all-gather.7.cloned.1.call-start = ((), (), s32[]{:S(2)}) async-start(), calls=%async_computation.6 | async-start | bytes 8912896 | tf_op jit(solution)/shard_map/all_gather | solution.py:29
  475.9 104.3 %all-gather.9.cloned.1.call-start = ((), (), s32[]{:S(2)}) async-start(), calls=%async_computation.9 | async-start | bytes 8912896 | tf_op jit(solution)/shard_map/all_gather | solution.py:29
  476.4 280.4 %reduce-scatter.7.cloned.1.call-start = ((), (), s32[]{:S(2)}) async-start(), calls=%async_computation.7 | async-start | bytes 17825792 | tf_op jit(solution)/shard_map/reduce_scatter | solution.py:38
  522.9 11.6 %copy-start.10 = (bf16[4096,1024]{1,0:T(8,128)(2,1)S(1)}, bf16[4096,1024]{1,0:T(8,128)(2,1)}, u32[]{:S(2)}) copy-start(bf16[4096,1024]{1,0:T(8,128)(2,1)} %all-gather.7.cloned.1.call-done) | copy-start | bytes 25165828
  579.4 0.7 copy-start.3
  579.4 0.7 copy-start.4
  579.4 355.2 %reduce-scatter.11.cloned.1.call-start = ((), (), s32[]{:S(2)}) async-start(), calls=%async_computation.10 | async-start | bytes 17825792 | tf_op jit(solution)/shard_map/reduce_scatter | solution.py:38
  580.2 11.6 %copy-start.9 = (bf16[4096,1024]{1,0:T(8,128)(2,1)S(1)}, bf16[4096,1024]{1,0:T(8,128)(2,1)}, u32[]{:S(2)}) copy-start(bf16[4096,1024]{1,0:T(8,128)(2,1)} %all-gather.9.cloned.1.call-done) | copy-start | bytes 25165828
  636.8 120.1 %copy-start.1 = (bf16[256,1024]{1,0:T(8,128)(2,1)S(1)}, bf16[256,1024]{1,0:T(8,128)(2,1)}, u32[]{:S(2)}) copy-start(bf16[256,1024]{1,0:T(8,128)(2,1)} %get-tuple-element.5) | copy-start | bytes 1572868
  636.8 297.9 %copy-start = (bf16[256,1024]{1,0:T(8,128)(2,1)S(1)}, bf16[256,1024]{1,0:T(8,128)(2,1)}, u32[]{:S(2)}) copy-start(bf16[256,1024]{1,0:T(8,128)(2,1)} %get-tuple-element.6) | copy-start | bytes 1572868
Sparse Core Ops, SparseCore 0:
  9.6 51.4 all-gather.12
  63.3 48.6 all-gather.10
  118.0 177.2 reduce-scatter.8
  297.4 175.4 reduce-scatter.4
  476.0 46.8 all-gather.6
  525.0 48.6 all-gather.8
  579.6 177.2 reduce-scatter.6
  759.1 175.4 reduce-scatter.10

commit v2 on v1

v2 whole, which is shorter than its diff:
```python
import functools

import jax
import jax.numpy as jnp
from jax import lax
from jax.experimental import pallas as pl
from jax.experimental.pallas import tpu as pltpu
from jax.sharding import PartitionSpec as P

ROUTE_SCALE = 2.5
MESH_AXES = ("ez", "ey", "ex")
MESH = pl.DeviceIdType.MESH
BF16, F32 = jnp.bfloat16, jnp.float32

TOK, HID, FFN = 256, 1024, 512
PARTS = (96, 80, 80)
OFFS = (0, 96, 176)
HALF = 4 * TOK
CHUNK = 256
CHUNKS = 8 * TOK // CHUNK
STAGES = 4

AXES_OF = tuple(((k + 2) % 3, (k + 1) % 3, k) for k in range(3))
GATHER = ((0, 1, 2), (0, 2, 1), (0, 4, 0), (1, 3, 1), (1, 5, 0), (2, 6, 0), (3, 7, 0))


def base(place, k):
    return (place // 4) * HALF + 4 * OFFS[k] + (place % 4) * PARTS[k]


def bits_of(place, k):
    bits = [0, 0, 0]
    for weight, axis in zip((4, 2, 1), AXES_OF[k]):
        bits[axis] = 1 if place & weight else 0
    return bits


def moe_kernel(tok, ids, gts, w1h, w3h, w2h, out, xbuf, pbuf, ra, rb, rc, w1, w3, w2, tt, gr, gbuf, fin,
               ag_s, ag_r, rs_s, rs_r, wl_s, wr_s, wr_r, g_s, g_r, t_s, o_s, credit, wfree):
    z, y, ex = (lax.axis_index(name) for name in MESH_AXES)
    x, core = ex // 2, ex % 2

    def dev(bx, by, bz):
        xx = 1 - x if bx else x
        return (1 - z if bz else z, 1 - y if by else y, xx * 2 + core)

    nbr = (dev(1, 0, 0), dev(0, 1, 0), dev(0, 0, 1))
    sib = (z, y, x * 2 + 1 - core)

    def remote(src, dst, ss, rs, to):
        return pltpu.make_async_remote_copy(src_ref=src, dst_ref=dst, send_sem=ss, recv_sem=rs, device_id=to, device_id_type=MESH)

    def ag(s, k, j):
        src, dst, which = GATHER[j]
        par = s % 2
        return remote(xbuf.at[par, pl.ds(base(src, k), PARTS[k])], xbuf.at[par, pl.ds(base(dst, k), PARTS[k])],
                      ag_s.at[par, k, j], ag_r.at[par, k, j], nbr[AXES_OF[k][which]])

    def rs(s, k, j):
        par, r = s % 2, PARTS[k]
        if j == 0:
            src, dst, which = pbuf.at[par, pl.ds(base(6, k), 2 * r)], ra.at[par, pl.ds(base(2, k), 2 * r)], 0
        elif j == 1:
            src, dst, which = pbuf.at[par, pl.ds(base(4, k), 2 * r)], ra.at[par, pl.ds(base(0, k), 2 * r)], 0
        elif j == 2:
            src, dst, which = pbuf.at[par, pl.ds(base(3, k), r)], rb.at[par, pl.ds(2 * OFFS[k] + r, r)], 1
        elif j == 3:
            src, dst, which = pbuf.at[par, pl.ds(base(2, k), r)], rb.at[par, pl.ds(2 * OFFS[k], r)], 1
        else:
            src, dst, which = pbuf.at[par, pl.ds(base(1, k), r)], rc.at[par, pl.ds(OFFS[k], r)], 2
        return remote(src, dst, rs_s.at[par, k, j], rs_r.at[par, k, j], nbr[AXES_OF[k][which]])

    def tok_load(mb, k):
        return pltpu.make_async_copy(tok.at[mb, pl.ds(OFFS[k], PARTS[k])], xbuf.at[mb, pl.ds(base(0, k), PARTS[k])], t_s.at[mb, k])

    def out_store(mb, k):
        rows = pl.ds(OFFS[k], PARTS[k])
        return pltpu.make_async_copy(fin.at[mb, rows], out.at[mb, rows], o_s.at[mb, k])

    def w_local(layer):
        return [pltpu.make_async_copy(h.at[layer], v.at[pl.ds(0, 2)], wl_s.at[i]) for i, (h, v) in enumerate(((w1h, w1), (w3h, w3), (w2h, w2)))]

    def w_remote(layer):
        return [remote(h.at[layer], v.at[pl.ds(2, 2)], wr_s.at[i], wr_r.at[i], sib) for i, (h, v) in enumerate(((w1h, w1), (w3h, w3), (w2h, w2)))]

    def gate_copy(r):
        bx, by, bz = r & 1, (r >> 1) & 1, (r >> 2) & 1
        rows = pl.ds(16 * r, 16)
        return remote(tt.at[rows], gr.at[rows], g_s.at[r], g_r.at[r], dev(bx, by, bz))

    def ag_begin(s, k):
        for j in range(3):
            ag(s, k, j).start()

    def f1(s):
        for k in range(3):
            ag(s, k, 0).wait_recv()
            ag(s, k, 3).start()
            ag(s, k, 4).start()

    def f2(s):
        for k in range(3):
            ag(s, k, 1).wait_recv()
            ag(s, k, 5).start()

    def f3(s):
        for k in range(3):
            ag(s, k, 3).wait_recv()
            ag(s, k, 6).start()

    def far(s, k):
        for j in (2, 4, 5, 6):
            ag(s, k, j).wait_recv()

    def ag_sent(s):
        for k in range(3):
            for j in range(7):
                ag(s, k, j).wait_send()

    def rs_sent(s):
        for k in range(3):
            for j in range(5):
                rs(s, k, j).wait_send()

    def send_far(s, k):
        rs(s, k, 0).start()
        rs(s, k, 1).start()

    def add(s, place, k, n, src):
        rows = pl.ds(base(place, k), n)
        pbuf[s % 2, rows] = pbuf[s % 2, rows] + src

    def r1(s, k):
        r = PARTS[k]
        rs(s, k, 0).wait_recv()
        add(s, 2, k, 2 * r, ra[s % 2, pl.ds(base(2, k), 2 * r)])
        rs(s, k, 2).start()
        rs(s, k, 3).start()

    def r2(s, k):
        r = PARTS[k]
        rs(s, k, 1).wait_recv()
        add(s, 0, k, 2 * r, ra[s % 2, pl.ds(base(0, k), 2 * r)])

    def r3(s, k):
        r = PARTS[k]
        rs(s, k, 2).wait_recv()
        add(s, 1, k, r, rb[s % 2, pl.ds(2 * OFFS[k] + r, r)])
        rs(s, k, 4).start()

    def r45(s, k):
        par, r = s % 2, PARTS[k]
        rs(s, k, 3).wait_recv()
        rs(s, k, 4).wait_recv()
        rows = pl.ds(base(0, k), r)
        total = pbuf[par, rows] + rb[par, pl.ds(2 * OFFS[k], r)] + rc[par, pl.ds(OFFS[k], r)]
        new = (xbuf[par, rows].astype(F32) + ROUTE_SCALE * total).astype(BF16)
        if s < 2:
            xbuf[par, rows] = new
            ag_begin(s + 2, k)
        else:
            fin[par, pl.ds(OFFS[k], r)] = new
            out_store(par, k).start()

    def give_credit():
        for d in range(3):
            pl.semaphore_signal(credit.at[d], inc=1, device_id=nbr[d], device_id_type=MESH)

    def take_credit():
        for d in range(3):
            pl.semaphore_wait(credit.at[d], 1)

    for mb in range(2):
        for k in range(3):
            tok_load(mb, k).start()
    for cp in w_local(0):
        cp.start()
    barrier = pltpu.get_barrier_semaphore()
    for r in range(1, 8):
        pl.semaphore_signal(barrier, inc=1, device_id=dev(r & 1, (r >> 1) & 1, (r >> 2) & 1), device_id_type=MESH)
    pl.semaphore_signal(barrier, inc=1, device_id=sib, device_id_type=MESH)
    pl.semaphore_wait(barrier, 8)
    for k in range(3):
        tok_load(0, k).wait()
        ag_begin(0, k)
    for cp in w_remote(0):
        cp.start()

    lane = lax.broadcasted_iota(jnp.int32, (32, 128), 1)
    rel = lane // 16
    bx, by, bz = rel % 2, (rel // 2) % 2, rel // 4
    chip = (x + bx - 2 * x * bx) + 2 * (y + by - 2 * y * by) + 4 * (z + bz - 2 * z * bz)
    expert = 4 * chip + (lane % 4 + 2 * core) % 4
    stage_of = (lane % 16) // 4
    wanted = [jnp.where(stage_of == s, expert, -1) for s in range(STAGES)]

    def table_rows(i, _):
        acc = jnp.zeros((32, 128), F32)
        for s in range(STAGES):
            rows = pl.ds(pl.multiple_of(s * TOK + i * 32, 32), 32)
            id_blk, gt_blk = ids[rows, :], gts[rows, :]
            for j in range(8):
                acc = jnp.where(wanted[s] == id_blk[:, j:j + 1], gt_blk[:, j:j + 1], acc)
        gbuf[pl.ds(pl.multiple_of(i * 32, 32), 32), :] = acc
        return 0

    lax.fori_loop(0, TOK // 32, table_rows, 0)
    tt[...] = gbuf[pl.ds(0, TOK), :].T
    for r in range(1, 8):
        gate_copy(r).start()
    gr[pl.ds(0, 16)] = tt[pl.ds(0, 16)]

    f1(0)
    f2(0)
    f3(0)
    for k in range(3):
        tok_load(1, k).wait()
        ag_begin(1, k)
    for r in range(1, 8):
        gate_copy(r).wait()
    by_token = gr[...].T
    for k in range(3):
        for place in range(8):
            bits = bits_of(place, k)
            r = bits[0] + 2 * bits[1] + 4 * bits[2]
            piece = by_token[OFFS[k]:OFFS[k] + PARTS[k], :]
            gbuf[pl.ds(base(place, k), PARTS[k]), :] = pltpu.roll(piece, (128 - 16 * r) % 128, axis=1) if r else piece
    for cp in w_local(0) + w_remote(0):
        cp.wait()

    def after_layer_one():
        send_far(1, 2)
        ag_sent(1)
        give_credit()
        pl.semaphore_signal(wfree, inc=1, device_id=sib, device_id_type=MESH)
        for cp in w_local(1):
            cp.start()
        pl.semaphore_wait(wfree, 1)
        for cp in w_remote(1):
            cp.start()
        for k in range(3):
            r3(0, k)
        take_credit()
        for k in range(3):
            r45(0, k)
        for k in range(3):
            r1(1, k)
        f1(2)
        f2(2)
        for k in range(3):
            r2(1, k)
        f3(2)
        for cp in w_local(1) + w_remote(1):
            cp.wait()
        rs_sent(0)

    def each(step, s):
        for k in range(3):
            step(s, k)

    def begin_last():
        take_credit()
        each(r45, 1)

    plan = {
        4: [lambda: far(0, 0), lambda: f1(1)],
        5: [lambda: far(0, 1), lambda: f2(1)],
        6: [lambda: far(0, 2), lambda: send_far(0, 0), lambda: f3(1)],
        7: [lambda: send_far(0, 1)],
        8: [lambda: send_far(0, 2), lambda: ag_sent(0), give_credit],
        12: [lambda: each(r1, 0), lambda: far(1, 0)],
        13: [lambda: far(1, 1)],
        14: [lambda: far(1, 2), lambda: send_far(1, 0)],
        15: [lambda: send_far(1, 1), lambda: each(r2, 0)],
        16: [after_layer_one],
        17: [lambda: each(r3, 1)],
        18: [begin_last],
        20: [lambda: far(2, 0)],
        21: [lambda: far(2, 1), lambda: f1(3)],
        22: [lambda: far(2, 2), lambda: send_far(2, 0), lambda: f2(3)],
        23: [lambda: send_far(2, 1), lambda: f3(3)],
        24: [lambda: send_far(2, 2), lambda: ag_sent(2), lambda: rs_sent(1)],
        26: [lambda: each(r1, 2)],
        28: [lambda: far(3, 0)],
        29: [lambda: far(3, 1), lambda: each(r2, 2)],
        30: [lambda: far(3, 2), lambda: send_far(3, 0)],
        31: [lambda: send_far(3, 1), lambda: each(r3, 2)],
    }

    chunk_lane = lax.broadcasted_iota(jnp.int32, (CHUNK, 128), 1)

    def chunk(n, _):
        for when, steps in plan.items():
            @pl.when(n == when)
            def _():
                for step in steps:
                    step()
        stage = n // CHUNKS
        par = stage % 2
        rows = pl.ds(pl.multiple_of((n % CHUNKS) * CHUNK, CHUNK), CHUNK)
        x_blk = xbuf[par, rows, :]
        g_blk = gbuf[rows, :]
        for e in range(4):
            a = jnp.dot(x_blk, w1[e], preferred_element_type=F32)
            b = jnp.dot(x_blk, w3[e], preferred_element_type=F32)
            h = (jax.nn.silu(a) * b).astype(BF16)
            o = jnp.dot(h, w2[e], preferred_element_type=F32).astype(BF16).astype(F32)
            g = jnp.sum(jnp.where(chunk_lane == stage * 4 + e, g_blk, 0.0), axis=1, keepdims=True)
            term = jnp.where(g > 0.0, g * o, 0.0)
            pbuf[par, rows, :] = term if e == 0 else pbuf[par, rows, :] + term
        return 0

    lax.fori_loop(0, STAGES * CHUNKS, chunk, 0)
    send_far(3, 2)
    each(r45, 2)
    each(r1, 3)
    each(r2, 3)
    each(r3, 3)
    each(r45, 3)
    ag_sent(3)
    rs_sent(2)
    rs_sent(3)
    for mb in range(2):
        for k in range(3):
            out_store(mb, k).wait()


def solution(mesh):
    tok_spec = P(None, MESH_AXES, None)
    route_spec = P(None, None, MESH_AXES, None)
    weight_spec = P(None, MESH_AXES, None, None)

    def device_body(tokens_in, expert_ids, gate_vals, w_up1, w_up3, w_down):
        any_spec = pl.BlockSpec(memory_space=pl.ANY)
        vmem_spec = pl.BlockSpec(memory_space=pltpu.VMEM)
        dma = pltpu.SemaphoreType.DMA
        return pl.pallas_call(
            moe_kernel,
            name="moe_layers",
            out_shape=jax.ShapeDtypeStruct(tokens_in.shape, BF16),
            in_specs=[any_spec, vmem_spec, vmem_spec, any_spec, any_spec, any_spec],
            out_specs=any_spec,
            scratch_shapes=[
                pltpu.VMEM((2, 8 * TOK, HID), BF16),
                pltpu.VMEM((2, 8 * TOK, HID), F32),
                pltpu.VMEM((2, HALF, HID), F32),
                pltpu.VMEM((2, 2 * TOK, HID), F32),
                pltpu.VMEM((2, TOK, HID), F32),
                pltpu.VMEM((4, HID, FFN), BF16),
                pltpu.VMEM((4, HID, FFN), BF16),
                pltpu.VMEM((4, FFN, HID), BF16),
                pltpu.VMEM((128, TOK), F32),
                pltpu.VMEM((128, TOK), F32),
                pltpu.VMEM((8 * TOK, 128), F32),
                pltpu.VMEM((2, TOK, HID), BF16),
                dma((2, 3, 7)), dma((2, 3, 7)), dma((2, 3, 5)), dma((2, 3, 5)),
                dma((3,)), dma((3,)), dma((3,)), dma((8,)), dma((8,)), dma((2, 3)), dma((2, 3)),
                pltpu.SemaphoreType.REGULAR((3,)), pltpu.SemaphoreType.REGULAR,
            ],
            compiler_params=pltpu.CompilerParams(collective_id=0, has_side_effects=True, vmem_limit_bytes=66 * 10**6),
        )(tokens_in, expert_ids.reshape(-1, expert_ids.shape[-1]), gate_vals.reshape(-1, gate_vals.shape[-1]), w_up1, w_up3, w_down)

    return jax.shard_map(device_body, mesh=mesh, in_specs=(tok_spec, route_spec, route_spec, weight_spec, weight_spec, weight_spec), out_specs=tok_spec, check_vma=False)
```

time: 953 us -> 350 us (0.37)
  waiting for transfers between devices: 680 us -> 0 us
  Pallas kernels: 0 us -> 344 us
  matrix products: 227 us -> 0 us
  between operations: 14 us -> 0.01 us
  blocking collectives: 11.4 us -> 0 us
    reduce_scatter x4 -> x0, waiting for transfers between devices: 594 us -> none  [device_body(): lax.psum_scatter(total, MESH_AXES, scatter_dimension=0, tiled=True)]
    pallas_call x0 -> x1, Pallas kernels: none -> 344 us  [device_body(): pl.pallas_call(moe_kernel, name='moe_layers', out_shape=jax.ShapeDtypeStr...]
    dot_general x16 -> x0, matrix products: 227 us -> none  [the longest x8 148 us: device_body(): jnp.dot(h, w_down[layer_idx, e], preferred_element_type=jnp.float32)]
    all_gather x4 -> x0, waiting for transfers between devices: 84.3 us -> none  [device_body(): everyone = lax.all_gather(tokens, MESH_AXES, axis=0, tiled=True)]
    all_to_all x1 -> x0, blocking collectives: 11.4 us -> none  [device_body(): table = lax.all_to_all(table, MESH_AXES, 3, 2, tiled=True)]
  transfers between devices with their start and end apart: 8 -> 0, of which waited for: 6 -> 0; matrix products, arithmetic and copies ran while one was open for 24% -> 0% of each run, Pallas kernels for 0% -> 0%
where the time goes in v2:
time: 350 us; the launch traced here: 349 us
  Pallas kernels  344 us (98%)
  local copies, waits for them, and re-layouts  5.8 us (2%)
    pallas_call x1, Pallas kernels, device_body(): pl.pallas_call(moe_kernel, name='moe_layers', out_shape=jax.ShapeDtypeStr...  344 us

profile of v2, /device:TPU:0, one launch (start us, length us, event | category | flops | bytes accessed | tf_op | source)
XLA Modules:
  0.0 349.4 jit_solution(4204676040016956410)
XLA Ops:
  0.0 1.8 copy.7
  1.8 1.8 copy.8
  3.5 343.6 %moe_layers.1 = bf16[2,256,1024]{2,1,0:T(8,128)(2,1)} custom-call(bf16[2,256,1024]{2,1,0:T(8,128)(2,1)} %tok.1, s32[1024,8]{1,0:T(8,128)} %bitcast.2, f32[1024,8]{1,0:T(8,128)} %bitcast.3, bf16[2,2,1024,512]{3,2,1,0:T(8,128)(2,1)} %w1h.1, bf16[2,2,1024,512]{3,2,1,0:T(8,128)(2,1)} %w3h.1, bf16[2,2,512,1024]{3,2,1,0:T(8,128)(2,1)} %w2h.1), custom_call_target="tpu_custom_call" | custom-call | tf_op jit(solution)/shard_map/moe_layers/pallas_call | solution.py:337
  347.2 2.3 copy.10

commit v3 on v1

v3 whole, which is shorter than its diff:
```python
import jax
import jax.numpy as jnp
from jax import lax
from jax.experimental import pallas as pl
from jax.experimental.pallas import tpu as pltpu
from jax.sharding import PartitionSpec as P

ROUTE_SCALE = 2.5
MESH_AXES = ("ez", "ey", "ex")
MESH = pl.DeviceIdType.MESH
BF16, F32 = jnp.bfloat16, jnp.float32

TOK, HID, FFN = 256, 1024, 512
PART = TOK // 2
CHUNK = 256
PIECES = 4

AXES1 = (((0, 2, 1), (1, 2, 0)), ((0, 2, 1), (1, 0, 2)))
AXES2 = ((0, 1), (1, 0))
GATHER1 = ((0, 2, 1), (0, 1, 2), (0, 4, 0), (2, 3, 2), (2, 6, 0), (1, 5, 0), (3, 7, 0))
GATHER2 = ((0, 1, 1), (0, 2, 0), (1, 3, 0))


def base1(place, k):
    return (place // 4) * 4 * TOK + k * 4 * PART + (place % 4) * PART


def base2(place, k):
    return (place // 2) * 2 * TOK + k * 2 * PART + (place % 2) * PART


def block_of(place, axes):
    n = len(axes)
    return sum(((place >> (n - 1 - i)) & 1) << axis for i, axis in enumerate(axes))


def moe_kernel(tok, ids, gts, w1h, w3h, w2h, out, f1h, f3h, f2h, xbuf, x2, pbuf, ra, rb, rc, w1, w3, w2, tt, gr, gbuf, g2, fin,
               ag_s, ag_r, rs_s, rs_r, bg_s, bg_r, bs_s, bs_r, wl_s, wr_s, wr_r, wb_s, wb_r, z_s, z_r, fw_s, fw_r, g_s, g_r, t_s, o_s):
    z, y, ex = (lax.axis_index(name) for name in MESH_AXES)
    x, core = ex // 2, ex % 2

    def turned(bu, bv):
        return bu + core * (bv - bu), bv + core * (bu - bv)

    def dev(bu, bv, bz):
        bx, by = turned(bu, bv)
        return (z + bz - 2 * z * bz, y + by - 2 * y * by, (x + bx - 2 * x * bx) * 2 + core)

    nbr = (dev(1, 0, 0), dev(0, 1, 0), dev(0, 0, 1))
    sib = (z, y, x * 2 + 1 - core)

    def remote(src, dst, ss, rs, to):
        return pltpu.make_async_remote_copy(src_ref=src, dst_ref=dst, send_sem=ss, recv_sem=rs, device_id=to, device_id_type=MESH)

    def ag(s, k, j):
        src, dst, which = GATHER1[j]
        return remote(xbuf.at[s, pl.ds(base1(src, k), PART)], xbuf.at[s, pl.ds(base1(dst, k), PART)],
                      ag_s.at[s, k, j], ag_r.at[s, k, j], nbr[AXES1[s][k][which]])

    def rs(s, k, j):
        if j < 2:
            src, dst, which = pbuf.at[s, pl.ds(base1(6 - 2 * j, k), 2 * PART)], ra.at[s, pl.ds((4 * k + 2 - 2 * j) * PART, 2 * PART)], 0
        elif j < 4:
            src, dst, which = pbuf.at[s, pl.ds(base1(7 - 2 * j, k), PART)], rb.at[s, pl.ds((2 * k + 3 - j) * PART, PART)], 2
        else:
            src, dst, which = pbuf.at[s, pl.ds(base1(2, k), PART)], rc.at[s, pl.ds(k * PART, PART)], 1
        return remote(src, dst, rs_s.at[s, k, j], rs_r.at[s, k, j], nbr[AXES1[s][k][which]])

    def bg(s, k, j):
        src, dst, which = GATHER2[j]
        return remote(x2.at[s, pl.ds(base2(src, k), PART)], x2.at[s, pl.ds(base2(dst, k), PART)],
                      bg_s.at[s, k, j], bg_r.at[s, k, j], nbr[AXES2[k][which]])

    def bs(s, k, j):
        if j < 2:
            src, dst, which = pbuf.at[s, pl.ds(base2(3 - j, k), PART)], ra.at[s, pl.ds((4 * k + 1 - j) * PART, PART)], 0
        else:
            src, dst, which = pbuf.at[s, pl.ds(base2(1, k), PART)], rb.at[s, pl.ds(2 * k * PART, PART)], 1
        return remote(src, dst, bs_s.at[s, k, j], bs_r.at[s, k, j], nbr[AXES2[k][which]])

    def tok_load(mb, k):
        return pltpu.make_async_copy(tok.at[mb, pl.ds(k * PART, PART)], xbuf.at[mb, pl.ds(base1(0, k), PART)], t_s.at[mb, k])

    def out_store(mb, k):
        rows = pl.ds(k * PART, PART)
        return pltpu.make_async_copy(fin.at[mb, rows], out.at[mb, rows], o_s.at[mb, k])

    held = ((w1h, f1h, w1), (w3h, f3h, w3), (w2h, f2h, w2))

    def w_first_local():
        return [pltpu.make_async_copy(h.at[0, e], v.at[e], wl_s.at[e, i]) for e in range(2) for i, (h, _, v) in enumerate(held)]

    def w_first_remote():
        return [remote(h.at[0], v.at[pl.ds(2, 2)], wr_s.at[i], wr_r.at[i], sib) for i, (h, _, v) in enumerate(held)]

    def w_second_swap():
        return [remote(h.at[1], f.at[pl.ds(0, 2)], wb_s.at[i], wb_r.at[i], sib) for i, (h, f, _) in enumerate(held)]

    def w_piece(p):
        e, i, q = p // (3 * PIECES), (p // PIECES) % 3, p % PIECES
        h, f, _ = held[i]
        rows = pl.ds(q * (h.shape[2] // PIECES), h.shape[2] // PIECES)
        return remote(h.at[1, e, rows], f.at[2 + e, rows], z_s.at[p], z_r.at[p], nbr[2])

    def w_forward(e):
        return [remote(f.at[2 + e], f.at[4 + e], fw_s.at[e, i], fw_r.at[e, i], sib) for i, (_, f, _) in enumerate(held)]

    def w_load(zc, slot):
        if zc:
            srcs = [f.at[2 + slot] for _, f, _ in held]
        else:
            srcs = [h.at[1, slot] if slot < 2 else f.at[slot - 2] for h, f, _ in held]
        return [pltpu.make_async_copy(src, held[i][2].at[slot], wl_s.at[slot, i]) for i, src in enumerate(srcs)]

    def start(copies):
        for cp in copies:
            cp.start()

    def wait(copies):
        for cp in copies:
            cp.wait()

    def wait_recv(copies):
        for cp in copies:
            cp.wait_recv()

    def pieces_in(e):
        wait_recv([w_piece(p) for p in range(e * 3 * PIECES, (e + 1) * 3 * PIECES)])

    fed = [0]

    def feed(n):
        while n and fed[0] < 6 * PIECES:
            w_piece(fed[0]).start()
            fed[0] += 1
            n -= 1

    gate_rows = [(16 * r, 16, r) for r in (1, 2, 3)] + [(16 * (r + 4) + 8, 8, r) for r in (1, 2, 3)] + [(16 * r, 8, r) for r in (4, 5, 6, 7)]

    def gate_copies():
        return [remote(tt.at[pl.ds(row, n)], gr.at[pl.ds(row, n)], g_s.at[i], g_r.at[i], dev(r & 1, (r >> 1) & 1, r >> 2))
                for i, (row, n, r) in enumerate(gate_rows)]

    def ag_begin(s, *js):
        for j in js:
            for k in range(2):
                ag(s, k, j).start()

    def f1(s):
        for k in range(2):
            ag(s, k, 0).wait_recv()
            ag(s, k, 3).start()
            ag(s, k, 4).start()

    def f2(s):
        for k in range(2):
            ag(s, k, 1).wait_recv()
            ag(s, k, 5).start()

    def f3(s):
        for k in range(2):
            ag(s, k, 3).wait_recv()
            ag(s, k, 6).start()

    def far(s, k):
        for j in (2, 4, 5, 6):
            ag(s, k, j).wait_recv()

    def add(s, row, n, src):
        rows = pl.ds(row, n)
        pbuf[s, rows] = pbuf[s, rows] + src

    def r1(s):
        for k in range(2):
            rs(s, k, 0).wait_recv()
            add(s, base1(2, k), 2 * PART, ra[s, pl.ds((4 * k + 2) * PART, 2 * PART)])
            rs(s, k, 2).start()

    def r2(s):
        for k in range(2):
            rs(s, k, 1).wait_recv()
            add(s, base1(0, k), 2 * PART, ra[s, pl.ds(4 * k * PART, 2 * PART)])
            rs(s, k, 3).start()

    def r3(s):
        for k in range(2):
            rs(s, k, 2).wait_recv()
            add(s, base1(2, k), PART, rb[s, pl.ds((2 * k + 1) * PART, PART)])
            rs(s, k, 4).start()

    def r45(s):
        for k in range(2):
            rs(s, k, 3).wait_recv()
            rs(s, k, 4).wait_recv()
            rows = pl.ds(base1(0, k), PART)
            total = pbuf[s, rows] + rb[s, pl.ds(2 * k * PART, PART)] + rc[s, pl.ds(k * PART, PART)]
            x2[s, pl.ds(base2(0, k), PART)] = (xbuf[s, rows].astype(F32) + ROUTE_SCALE * total).astype(BF16)
            bg(s, k, 0).start()
            bg(s, k, 1).start()

    def clear(s):
        for k in range(2):
            for j in range(5):
                rs(s, k, j).wait_send()
        pbuf[s, pl.ds(0, 4 * TOK)] = jnp.zeros((4 * TOK, HID), F32)

    def g1(s):
        for k in range(2):
            bg(s, k, 0).wait_recv()
            bg(s, k, 2).start()

    def g_far(s):
        for k in range(2):
            bg(s, k, 1).wait_recv()
            bg(s, k, 2).wait_recv()

    def b_far(s):
        for j in range(2):
            for k in range(2):
                bs(s, k, j).start()

    def b1(s):
        for k in range(2):
            bs(s, k, 0).wait_recv()
            add(s, base2(1, k), PART, ra[s, pl.ds((4 * k + 1) * PART, PART)])
            bs(s, k, 2).start()

    def b2(s):
        for k in range(2):
            bs(s, k, 1).wait_recv()
            bs(s, k, 2).wait_recv()
            rows = pl.ds(base2(0, k), PART)
            total = pbuf[s, rows] + ra[s, pl.ds(4 * k * PART, PART)] + rb[s, pl.ds(2 * k * PART, PART)]
            fin[s, pl.ds(k * PART, PART)] = (x2[s, rows].astype(F32) + ROUTE_SCALE * total).astype(BF16)
            out_store(s, k).start()

    for mb in range(2):
        for k in range(2):
            tok_load(mb, k).start()
    start(w_first_local())
    barrier = pltpu.get_barrier_semaphore()
    for r in range(1, 8):
        pl.semaphore_signal(barrier, inc=1, device_id=dev(r & 1, (r >> 1) & 1, (r >> 2) & 1), device_id_type=MESH)
    pl.semaphore_signal(barrier, inc=1, device_id=sib, device_id_type=MESH)
    pl.semaphore_wait(barrier, 8)
    wait([tok_load(0, 0), tok_load(0, 1)])
    ag_begin(0, 0, 2, 1)
    wait([tok_load(1, 0), tok_load(1, 1)])
    ag_begin(1, 0)
    start(w_first_remote())

    row = lax.broadcasted_iota(jnp.int32, (128, TOK), 0)
    rel = row // 16
    bx, by = turned(rel % 2, (rel // 2) % 2)
    bz = rel // 4
    chip = (x + bx - 2 * x * bx) + 2 * (y + by - 2 * y * by) + 4 * (z + bz - 2 * z * bz)
    expert = 4 * chip + (row % 4 + 2 * core) % 4
    table = jnp.zeros((128, TOK), F32)
    for s in range(4):
        wanted = jnp.where((row % 16) // 4 == s, expert, -1)
        for j in range(8):
            i = 8 * s + j
            table = jnp.where(wanted == ids[i:i + 1, :], gts[i:i + 1, :], table)
    tt[...] = table
    start(gate_copies())
    gr[pl.ds(0, 16)] = tt[pl.ds(0, 16)]
    gr[pl.ds(72, 8)] = tt[pl.ds(72, 8)]

    f1(0)
    f2(0)
    feed(2)
    wait(gate_copies())
    by_token = gr[...].T
    low = lax.broadcasted_iota(jnp.int32, (PART, 128), 1)
    for k in range(2):
        piece = by_token[k * PART:(k + 1) * PART, :]

        def lanes_from(lane, to):
            return pltpu.roll(piece, (to - lane) % 128, axis=1) if lane != to else piece

        for place in range(8):
            r0, r1_ = block_of(place, AXES1[0][k]), block_of(place, AXES1[1][k])
            gbuf[pl.ds(base1(place, k), PART), :] = jnp.where(low < 4, lanes_from(16 * r0, 0), lanes_from(16 * r1_, 0))
        for place in range(4):
            r = block_of(place, AXES2[k])
            g2[pl.ds(base2(place, k), PART), :] = jnp.where(low < 8, lanes_from(16 * r + 8, 0), lanes_from(16 * (r + 4) + 8, 8))
    wait(w_first_local() + w_first_remote())

    lane = lax.broadcasted_iota(jnp.int32, (CHUNK, 128), 1)

    def weighted(x_blk, g_blk, column, slot):
        a = jnp.dot(x_blk, w1[slot], preferred_element_type=F32)
        b = jnp.dot(x_blk, w3[slot], preferred_element_type=F32)
        h = (jax.nn.silu(a) * b).astype(BF16)
        o = jnp.dot(h, w2[slot], preferred_element_type=F32).astype(BF16).astype(F32)
        g = jnp.sum(jnp.where(lane == column, g_blk, 0.0), axis=1, keepdims=True)
        return jnp.where(g > 0.0, g * o, 0.0)

    def hooks(n, plan):
        for when in sorted(plan):
            @pl.when(n == when)
            def _():
                for step in plan[when]:
                    step()

    def send(s, k, j):
        return lambda: rs(s, k, j).start()

    plan1 = {n: [lambda: feed(1)] for n in range(16)}
    plan1[1] += [lambda: f3(0), lambda: ag_begin(1, 2, 1), lambda: f1(1)]
    plan1[4] += [lambda: far(0, 0)]
    plan1[5] += [lambda: f2(1)]
    plan1[6] += [lambda: f3(1), send(0, 0, 0), send(0, 0, 1), lambda: far(0, 1)]
    plan1[7] += [send(0, 1, 0)]
    plan1[8] += [send(0, 1, 1)]
    plan1[9] += [lambda: start(w_second_swap())]
    plan1[12] += [lambda: far(1, 0)]
    plan1[14] += [lambda: far(1, 1)]

    def layer1(n, _):
        hooks(n, plan1)
        s = n // 8
        c = n % 8
        c = c + (c // 4) * (1 - 2 * (c % 2))
        rows = pl.ds(pl.multiple_of(c * CHUNK, CHUNK), CHUNK)
        x_blk, g_blk = xbuf[s, rows, :], gbuf[rows, :]
        for e in range(4):
            term = weighted(x_blk, g_blk, s * 4 + e, e)
            pbuf[s, rows, :] = term if e == 0 else pbuf[s, rows, :] + term
        return 0

    lax.fori_loop(0, 16, layer1, 0)

    start(w_load(0, 0) + w_load(0, 1))
    r1(0)
    wait_recv(w_second_swap())
    start(w_load(0, 2) + w_load(0, 3))
    pieces_in(0)
    start(w_forward(0))
    r2(0)
    for k in range(2):
        rs(1, k, 0).start()
    r3(0)
    feed(1)
    r45(0)
    r1(1)
    feed(2)
    g1(0)
    for k in range(2):
        rs(1, k, 1).start()
    clear(0)
    r3(1)
    feed(2)
    for slot in range(4):
        wait(w_load(0, slot))
    g_far(0)

    def unit(s, half, zc, slot):
        for part in range(2):
            rows = pl.ds(pl.multiple_of(half * 2 * TOK + part * CHUNK, CHUNK), CHUNK)
            pbuf[s, rows, :] += weighted(x2[s, rows, :], g2[rows, :], zc * 8 + s * 4 + slot, slot)

    order = (0, 2, 1, 3)

    def load(zc, slot):
        return lambda: start(w_load(zc, slot))

    def loaded(zc, slot):
        return lambda: wait(w_load(zc, slot))

    plan2 = {
        2: [load(1, 0)],
        4: [lambda: wait_recv(w_forward(0)), load(1, 2)],
        8: [loaded(1, 0), lambda: r2(1), lambda: feed(24)],
        10: [loaded(1, 2)],
        11: [lambda: r45(1)],
    }

    def second_a(m, _):
        hooks(m, plan2)
        i = m // 2
        unit(0, 1 - m % 2, i // 4, (i % 2) * 2 + (i % 4) // 2)
        return 0

    lax.fori_loop(0, 12, second_a, 0)
    pieces_in(1)
    start(w_forward(1))
    load(1, 1)()
    clear(1)
    loaded(1, 1)()

    def arrived():
        wait_recv(w_forward(1))
        start(w_load(1, 3))
        g1(1)
        wait(w_load(1, 3))

    plan3 = {1: [arrived], 2: [lambda: b_far(0)]}

    def second_b(m, _):
        hooks(m, plan3)
        unit(0, 1 - m // 2, 1, 1 + 2 * (m % 2))
        return 0

    lax.fori_loop(0, 4, second_b, 0)
    g_far(1)

    plan4 = {}
    for i in range(4):
        plan4.setdefault(i + 1, []).append(load(0, order[i]))
        plan4.setdefault(i + 9, []).append(load(1, order[i]))
        plan4.setdefault(i + 4, []).append(loaded(0, order[i]))
        plan4.setdefault(i + 12, []).append(loaded(1, order[i]))
    plan4[6].append(lambda: b1(0))
    plan4.setdefault(8, []).append(lambda: b_far(1))

    def second_c(m, _):
        hooks(m, plan4)
        q, j = m // 4, m % 4
        unit(1, 1 - q // 2, 1 - ((q + 1) // 2) % 2, (j % 2) * 2 + j // 2)
        return 0

    lax.fori_loop(0, 16, second_c, 0)
    b2(0)
    b1(1)
    b2(1)
    for s in range(2):
        for k in range(2):
            for j in range(7):
                ag(s, k, j).wait_send()
            for j in range(3):
                bg(s, k, j).wait_send()
                bs(s, k, j).wait_send()
    for cp in w_second_swap() + w_forward(0) + w_forward(1) + [w_piece(p) for p in range(6 * PIECES)]:
        cp.wait_send()
    for mb in range(2):
        for k in range(2):
            out_store(mb, k).wait()


def solution(mesh):
    tok_spec = P(None, MESH_AXES, None)
    route_spec = P(None, None, MESH_AXES, None)
    weight_spec = P(None, MESH_AXES, None, None)

    def device_body(tokens_in, expert_ids, gate_vals, w_up1, w_up3, w_down):
        any_spec = pl.BlockSpec(memory_space=pl.ANY)
        vmem_spec = pl.BlockSpec(memory_space=pltpu.VMEM)
        dma = pltpu.SemaphoreType.DMA

        def by_slot(route):
            return jnp.swapaxes(route, 2, 3).reshape(-1, route.shape[2])

        return pl.pallas_call(
            moe_kernel,
            name="moe_layers",
            out_shape=[
                jax.ShapeDtypeStruct(tokens_in.shape, BF16),
                jax.ShapeDtypeStruct((6, HID, FFN), BF16),
                jax.ShapeDtypeStruct((6, HID, FFN), BF16),
                jax.ShapeDtypeStruct((6, FFN, HID), BF16),
            ],
            in_specs=[any_spec, vmem_spec, vmem_spec, any_spec, any_spec, any_spec],
            out_specs=[any_spec] * 4,
            scratch_shapes=[
                pltpu.VMEM((2, 8 * TOK, HID), BF16),
                pltpu.VMEM((2, 4 * TOK, HID), BF16),
                pltpu.VMEM((2, 8 * TOK, HID), F32),
                pltpu.VMEM((2, 4 * TOK, HID), F32),
                pltpu.VMEM((2, 2 * TOK, HID), F32),
                pltpu.VMEM((2, TOK, HID), F32),
                pltpu.VMEM((4, HID, FFN), BF16),
                pltpu.VMEM((4, HID, FFN), BF16),
                pltpu.VMEM((4, FFN, HID), BF16),
                pltpu.VMEM((128, TOK), F32),
                pltpu.VMEM((128, TOK), F32),
                pltpu.VMEM((8 * TOK, 128), F32),
                pltpu.VMEM((4 * TOK, 128), F32),
                pltpu.VMEM((2, TOK, HID), BF16),
                dma((2, 2, 7)), dma((2, 2, 7)), dma((2, 2, 5)), dma((2, 2, 5)),
                dma((2, 2, 3)), dma((2, 2, 3)), dma((2, 2, 3)), dma((2, 2, 3)),
                dma((4, 3)), dma((3,)), dma((3,)), dma((3,)), dma((3,)),
                dma((6 * PIECES,)), dma((6 * PIECES,)), dma((2, 3)), dma((2, 3)), dma((10,)), dma((10,)), dma((2, 2)), dma((2, 2)),
            ],
            compiler_params=pltpu.CompilerParams(collective_id=0, has_side_effects=True, vmem_limit_bytes=66 * 10**6),
        )(tokens_in, by_slot(expert_ids), by_slot(gate_vals), w_up1, w_up3, w_down)[0]

    return jax.shard_map(device_body, mesh=mesh, in_specs=(tok_spec, route_spec, route_spec, weight_spec, weight_spec, weight_spec), out_specs=tok_spec, check_vma=False)
```

time: 953 us -> 319 us (0.33)
  waiting for transfers between devices: 680 us -> 0 us
  Pallas kernels: 0 us -> 316 us
  matrix products: 227 us -> 0 us
  between operations: 14 us -> 0.01 us
  blocking collectives: 11.4 us -> 0 us
    reduce_scatter x4 -> x0, waiting for transfers between devices: 594 us -> none  [device_body(): lax.psum_scatter(total, MESH_AXES, scatter_dimension=0, tiled=True)]
    pallas_call x0 -> x1, Pallas kernels: none -> 316 us  [device_body(): pl.pallas_call(moe_kernel, name='moe_layers', out_shape=[jax.ShapeDtypeSt...]
    dot_general x16 -> x0, matrix products: 227 us -> none  [the longest x8 148 us: device_body(): jnp.dot(h, w_down[layer_idx, e], preferred_element_type=jnp.float32)]
    all_gather x4 -> x0, waiting for transfers between devices: 84.3 us -> none  [device_body(): everyone = lax.all_gather(tokens, MESH_AXES, axis=0, tiled=True)]
    all_to_all x1 -> x0, blocking collectives: 11.4 us -> none  [device_body(): table = lax.all_to_all(table, MESH_AXES, 3, 2, tiled=True)]
  transfers between devices with their start and end apart: 8 -> 0, of which waited for: 6 -> 0; matrix products, arithmetic and copies ran while one was open for 24% -> 0% of each run, Pallas kernels for 0% -> 0%
where the time goes in v3:
time: 319 us
  Pallas kernels  316 us (99%)
    pallas_call x1, Pallas kernels, device_body(): pl.pallas_call(moe_kernel, name='moe_layers', out_shape=[jax.ShapeDtypeSt...  316 us

profile of v3, /device:TPU:0, one launch (start us, length us, event | category | flops | bytes accessed | tf_op | source)
XLA Modules:
  0.0 318.7 jit_solution(2557356690731321420)
XLA Ops:
  0.0 316.4 %moe_layers.1 = (bf16[2,256,1024]{2,1,0:T(8,128)(2,1)}, bf16[6,1024,512]{2,1,0:T(8,128)(2,1)}, bf16[6,1024,512]{2,1,0:T(8,128)(2,1)}, bf16[6,512,1024]{2,1,0:T(8,128)(2,1)}) custom-call(bf16[2,256,1024]{2,1,0:T(8,128)(2,1)} %tok.1, s32[32,256]{1,0:T(8,128)} %bitcast.6, f32[32,256]{1,0:T(8,128)} %bitcast.7, bf16[2,2,1024,512]{3,2,1,0:T(8,128)(2,1)} %w1h.1, ...), custom_call_target="tpu_custom_call" | custom-call | tf_op jit(solution)/shard_map/moe_layers/pallas_call | solution.py:454
  316.4 2.3 copy.8

commit v4 on v3

--- a/solution.py
+++ b/solution.py
@@ -11,18 +11,19 @@
 BF16, F32 = jnp.bfloat16, jnp.float32
 
 TOK, HID, FFN = 256, 1024, 512
-PART = TOK // 2
+N1, N2 = 4, 2
+ROW1, PART = TOK // N1, TOK // N2
 CHUNK = 256
 PIECES = 4
 
-AXES1 = (((0, 2, 1), (1, 2, 0)), ((0, 2, 1), (1, 0, 2)))
+AXES1 = (((0, 2, 1), (1, 2, 0)) * 2, ((0, 2, 1), (1, 2, 0), (0, 1, 2), (1, 0, 2)))
 AXES2 = ((0, 1), (1, 0))
 GATHER1 = ((0, 2, 1), (0, 1, 2), (0, 4, 0), (2, 3, 2), (2, 6, 0), (1, 5, 0), (3, 7, 0))
 GATHER2 = ((0, 1, 1), (0, 2, 0), (1, 3, 0))
 
 
 def base1(place, k):
-    return (place // 4) * 4 * TOK + k * 4 * PART + (place % 4) * PART
+    return (place // 4) * 4 * TOK + k * 4 * ROW1 + (place % 4) * ROW1
 
 
 def base2(place, k):
@@ -54,16 +55,16 @@
 
     def ag(s, k, j):
         src, dst, which = GATHER1[j]
-        return remote(xbuf.at[s, pl.ds(base1(src, k), PART)], xbuf.at[s, pl.ds(base1(dst, k), PART)],
+        return remote(xbuf.at[s, pl.ds(base1(src, k), ROW1)], xbuf.at[s, pl.ds(base1(dst, k), ROW1)],
                       ag_s.at[s, k, j], ag_r.at[s, k, j], nbr[AXES1[s][k][which]])
 
     def rs(s, k, j):
         if j < 2:
-            src, dst, which = pbuf.at[s, pl.ds(base1(6 - 2 * j, k), 2 * PART)], ra.at[s, pl.ds((4 * k + 2 - 2 * j) * PART, 2 * PART)], 0
+            src, dst, which = pbuf.at[s, pl.ds(base1(6 - 2 * j, k), 2 * ROW1)], ra.at[s, pl.ds((4 * k + 2 - 2 * j) * ROW1, 2 * ROW1)], 0
         elif j < 4:
-            src, dst, which = pbuf.at[s, pl.ds(base1(7 - 2 * j, k), PART)], rb.at[s, pl.ds((2 * k + 3 - j) * PART, PART)], 2
+            src, dst, which = pbuf.at[s, pl.ds(base1(7 - 2 * j, k), ROW1)], rb.at[s, pl.ds((2 * k + 3 - j) * ROW1, ROW1)], 2
         else:
-            src, dst, which = pbuf.at[s, pl.ds(base1(2, k), PART)], rc.at[s, pl.ds(k * PART, PART)], 1
+            src, dst, which = pbuf.at[s, pl.ds(base1(2, k), ROW1)], rc.at[s, pl.ds(k * ROW1, ROW1)], 1
         return remote(src, dst, rs_s.at[s, k, j], rs_r.at[s, k, j], nbr[AXES1[s][k][which]])
 
     def bg(s, k, j):
@@ -78,8 +79,8 @@
             src, dst, which = pbuf.at[s, pl.ds(base2(1, k), PART)], rb.at[s, pl.ds(2 * k * PART, PART)], 1
         return remote(src, dst, bs_s.at[s, k, j], bs_r.at[s, k, j], nbr[AXES2[k][which]])
 
-    def tok_load(mb, k):
-        return pltpu.make_async_copy(tok.at[mb, pl.ds(k * PART, PART)], xbuf.at[mb, pl.ds(base1(0, k), PART)], t_s.at[mb, k])
+    def tok_load(mb):
+        return [pltpu.make_async_copy(tok.at[mb, pl.ds(k * ROW1, ROW1)], xbuf.at[mb, pl.ds(base1(0, k), ROW1)], t_s.at[mb, k]) for k in range(N1)]
 
     def out_store(mb, k):
         rows = pl.ds(k * PART, PART)
@@ -143,24 +144,23 @@
 
     def ag_begin(s, *js):
         for j in js:
-            for k in range(2):
+            for k in range(N1):
                 ag(s, k, j).start()
 
     def f1(s):
-        for k in range(2):
+        for k in range(N1):
             ag(s, k, 0).wait_recv()
             ag(s, k, 3).start()
             ag(s, k, 4).start()
 
     def f2(s):
-        for k in range(2):
+        for k in range(N1):
             ag(s, k, 1).wait_recv()
             ag(s, k, 5).start()
 
-    def f3(s):
-        for k in range(2):
-            ag(s, k, 3).wait_recv()
-            ag(s, k, 6).start()
+    def f3(s, k):
+        ag(s, k, 3).wait_recv()
+        ag(s, k, 6).start()
 
     def far(s, k):
         for j in (2, 4, 5, 6):
@@ -171,35 +171,37 @@
         pbuf[s, rows] = pbuf[s, rows] + src
 
     def r1(s):
-        for k in range(2):
+        for k in range(N1):
             rs(s, k, 0).wait_recv()
-            add(s, base1(2, k), 2 * PART, ra[s, pl.ds((4 * k + 2) * PART, 2 * PART)])
+            add(s, base1(2, k), 2 * ROW1, ra[s, pl.ds((4 * k + 2) * ROW1, 2 * ROW1)])
             rs(s, k, 2).start()
 
     def r2(s):
-        for k in range(2):
+        for k in range(N1):
             rs(s, k, 1).wait_recv()
-            add(s, base1(0, k), 2 * PART, ra[s, pl.ds(4 * k * PART, 2 * PART)])
+            add(s, base1(0, k), 2 * ROW1, ra[s, pl.ds(4 * k * ROW1, 2 * ROW1)])
             rs(s, k, 3).start()
 
     def r3(s):
-        for k in range(2):
+        for k in range(N1):
             rs(s, k, 2).wait_recv()
-            add(s, base1(2, k), PART, rb[s, pl.ds((2 * k + 1) * PART, PART)])
+            add(s, base1(2, k), ROW1, rb[s, pl.ds((2 * k + 1) * ROW1, ROW1)])
             rs(s, k, 4).start()
 
     def r45(s):
-        for k in range(2):
+        for k in range(N1):
             rs(s, k, 3).wait_recv()
             rs(s, k, 4).wait_recv()
-            rows = pl.ds(base1(0, k), PART)
-            total = pbuf[s, rows] + rb[s, pl.ds(2 * k * PART, PART)] + rc[s, pl.ds(k * PART, PART)]
-            x2[s, pl.ds(base2(0, k), PART)] = (xbuf[s, rows].astype(F32) + ROUTE_SCALE * total).astype(BF16)
-            bg(s, k, 0).start()
-            bg(s, k, 1).start()
+            rows = pl.ds(base1(0, k), ROW1)
+            total = pbuf[s, rows] + rb[s, pl.ds(2 * k * ROW1, ROW1)] + rc[s, pl.ds(k * ROW1, ROW1)]
+            into = base2(0, k * N2 // N1) + (k * ROW1) % PART
+            x2[s, pl.ds(into, ROW1)] = (xbuf[s, rows].astype(F32) + ROUTE_SCALE * total).astype(BF16)
+            if (k + 1) * ROW1 % PART == 0:
+                bg(s, k * N2 // N1, 0).start()
+                bg(s, k * N2 // N1, 1).start()
 
     def clear(s):
-        for k in range(2):
+        for k in range(N1):
             for j in range(5):
                 rs(s, k, j).wait_send()
         pbuf[s, pl.ds(0, 4 * TOK)] = jnp.zeros((4 * TOK, HID), F32)
@@ -234,18 +236,16 @@
             fin[s, pl.ds(k * PART, PART)] = (x2[s, rows].astype(F32) + ROUTE_SCALE * total).astype(BF16)
             out_store(s, k).start()
 
-    for mb in range(2):
-        for k in range(2):
-            tok_load(mb, k).start()
+    start(tok_load(0) + tok_load(1))
     start(w_first_local())
     barrier = pltpu.get_barrier_semaphore()
     for r in range(1, 8):
         pl.semaphore_signal(barrier, inc=1, device_id=dev(r & 1, (r >> 1) & 1, (r >> 2) & 1), device_id_type=MESH)
     pl.semaphore_signal(barrier, inc=1, device_id=sib, device_id_type=MESH)
     pl.semaphore_wait(barrier, 8)
-    wait([tok_load(0, 0), tok_load(0, 1)])
+    wait(tok_load(0))
     ag_begin(0, 0, 2, 1)
-    wait([tok_load(1, 0), tok_load(1, 1)])
+    wait(tok_load(1))
     ag_begin(1, 0)
     start(w_first_remote())
 
@@ -271,19 +271,19 @@
     feed(2)
     wait(gate_copies())
     by_token = gr[...].T
-    low = lax.broadcasted_iota(jnp.int32, (PART, 128), 1)
-    for k in range(2):
-        piece = by_token[k * PART:(k + 1) * PART, :]
-
-        def lanes_from(lane, to):
-            return pltpu.roll(piece, (to - lane) % 128, axis=1) if lane != to else piece
-
+
+    def lanes(piece, first, second, cut):
+        spot = lax.broadcasted_iota(jnp.int32, piece.shape, 1)
+        return jnp.where(spot < cut, pltpu.roll(piece, (128 - first) % 128, axis=1), pltpu.roll(piece, (cut + 128 - second) % 128, axis=1))
+
+    for k in range(N1):
         for place in range(8):
-            r0, r1_ = block_of(place, AXES1[0][k]), block_of(place, AXES1[1][k])
-            gbuf[pl.ds(base1(place, k), PART), :] = jnp.where(low < 4, lanes_from(16 * r0, 0), lanes_from(16 * r1_, 0))
+            r_0, r_1 = block_of(place, AXES1[0][k]), block_of(place, AXES1[1][k])
+            gbuf[pl.ds(base1(place, k), ROW1), :] = lanes(by_token[k * ROW1:(k + 1) * ROW1, :], 16 * r_0, 16 * r_1 + 4, 4)
+    for k in range(N2):
         for place in range(4):
             r = block_of(place, AXES2[k])
-            g2[pl.ds(base2(place, k), PART), :] = jnp.where(low < 8, lanes_from(16 * r + 8, 0), lanes_from(16 * (r + 4) + 8, 8))
+            g2[pl.ds(base2(place, k), PART), :] = lanes(by_token[k * PART:(k + 1) * PART, :], 16 * r + 8, 16 * (r + 4) + 8, 8)
     wait(w_first_local() + w_first_remote())
 
     lane = lax.broadcasted_iota(jnp.int32, (CHUNK, 128), 1)
@@ -303,26 +303,25 @@
                 for step in plan[when]:
                     step()
 
-    def send(s, k, j):
-        return lambda: rs(s, k, j).start()
+    def send(k):
+        return lambda: start([rs(0, k, 0), rs(0, k, 1)])
 
     plan1 = {n: [lambda: feed(1)] for n in range(16)}
-    plan1[1] += [lambda: f3(0), lambda: ag_begin(1, 2, 1), lambda: f1(1)]
+    plan1[0] += [lambda: f3(0, 0)]
+    plan1[1] += [lambda: f3(0, 1), lambda: f3(0, 2), lambda: f3(0, 3), lambda: ag_begin(1, 2, 1), lambda: f1(1)]
     plan1[4] += [lambda: far(0, 0)]
-    plan1[5] += [lambda: f2(1)]
-    plan1[6] += [lambda: f3(1), send(0, 0, 0), send(0, 0, 1), lambda: far(0, 1)]
-    plan1[7] += [send(0, 1, 0)]
-    plan1[8] += [send(0, 1, 1)]
+    plan1[5] += [lambda: far(0, 1), lambda: f2(1)]
+    plan1[6] += [lambda: far(0, 2)] + [lambda k=k: f3(1, k) for k in range(N1)] + [send(0), send(1)]
+    plan1[7] += [lambda: far(0, 3), send(2)]
+    plan1[8] += [send(3)]
     plan1[9] += [lambda: start(w_second_swap())]
-    plan1[12] += [lambda: far(1, 0)]
-    plan1[14] += [lambda: far(1, 1)]
+    for k in range(N1):
+        plan1[12 + k] += [lambda k=k: far(1, k)]
 
     def layer1(n, _):
         hooks(n, plan1)
         s = n // 8
-        c = n % 8
-        c = c + (c // 4) * (1 - 2 * (c % 2))
-        rows = pl.ds(pl.multiple_of(c * CHUNK, CHUNK), CHUNK)
+        rows = pl.ds(pl.multiple_of((n % 8) * CHUNK, CHUNK), CHUNK)
         x_blk, g_blk = xbuf[s, rows, :], gbuf[rows, :]
         for e in range(4):
             term = weighted(x_blk, g_blk, s * 4 + e, e)
@@ -338,16 +337,14 @@
     pieces_in(0)
     start(w_forward(0))
     r2(0)
-    for k in range(2):
-        rs(1, k, 0).start()
+    start([rs(1, k, 0) for k in range(N1)])
     r3(0)
     feed(1)
     r45(0)
     r1(1)
     feed(2)
     g1(0)
-    for k in range(2):
-        rs(1, k, 1).start()
+    start([rs(1, k, 1) for k in range(N1)])
     clear(0)
     r3(1)
     feed(2)
@@ -425,12 +422,8 @@
     b1(1)
     b2(1)
     for s in range(2):
-        for k in range(2):
-            for j in range(7):
-                ag(s, k, j).wait_send()
-            for j in range(3):
-                bg(s, k, j).wait_send()
-                bs(s, k, j).wait_send()
+        for cp in [ag(s, k, j) for k in range(N1) for j in range(7)] + [c(s, k, j) for c in (bg, bs) for k in range(N2) for j in range(3)]:
+            cp.wait_send()
     for cp in w_second_swap() + w_forward(0) + w_forward(1) + [w_piece(p) for p in range(6 * PIECES)]:
         cp.wait_send()
     for mb in range(2):
@@ -477,10 +470,10 @@
                 pltpu.VMEM((8 * TOK, 128), F32),
                 pltpu.VMEM((4 * TOK, 128), F32),
                 pltpu.VMEM((2, TOK, HID), BF16),
-                dma((2, 2, 7)), dma((2, 2, 7)), dma((2, 2, 5)), dma((2, 2, 5)),
+                dma((2, N1, 7)), dma((2, N1, 7)), dma((2, N1, 5)), dma((2, N1, 5)),
                 dma((2, 2, 3)), dma((2, 2, 3)), dma((2, 2, 3)), dma((2, 2, 3)),
                 dma((4, 3)), dma((3,)), dma((3,)), dma((3,)), dma((3,)),
-                dma((6 * PIECES,)), dma((6 * PIECES,)), dma((2, 3)), dma((2, 3)), dma((10,)), dma((10,)), dma((2, 2)), dma((2, 2)),
+                dma((6 * PIECES,)), dma((6 * PIECES,)), dma((2, 3)), dma((2, 3)), dma((10,)), dma((10,)), dma((2, N1)), dma((2, 2)),
             ],
             compiler_params=pltpu.CompilerParams(collective_id=0, has_side_effects=True, vmem_limit_bytes=66 * 10**6),
         )(tokens_in, by_slot(expert_ids), by_slot(gate_vals), w_up1, w_up3, w_down)[0]

time: 319 us -> 313 us (0.981)
  Pallas kernels: 316 us -> 311 us
    pallas_call x1, Pallas kernels: 316 us -> 311 us  [device_body(): pl.pallas_call(moe_kernel, name='moe_layers', out_shape=[jax.ShapeDtypeSt...]
where the time goes in v4:
time: 313 us
  Pallas kernels  311 us (99%)
    pallas_call x1, Pallas kernels, device_body(): pl.pallas_call(moe_kernel, name='moe_layers', out_shape=[jax.ShapeDtypeSt...  311 us

profile of v4, /device:TPU:0, one launch (start us, length us, event | category | flops | bytes accessed | tf_op | source)
XLA Modules:
  0.0 313.0 jit_solution(11765451121899870367)
XLA Ops:
  0.0 310.7 %moe_layers.1 = (bf16[2,256,1024]{2,1,0:T(8,128)(2,1)}, bf16[6,1024,512]{2,1,0:T(8,128)(2,1)}, bf16[6,1024,512]{2,1,0:T(8,128)(2,1)}, bf16[6,512,1024]{2,1,0:T(8,128)(2,1)}) custom-call(bf16[2,256,1024]{2,1,0:T(8,128)(2,1)} %tok.1, s32[32,256]{1,0:T(8,128)} %bitcast.6, f32[32,256]{1,0:T(8,128)} %bitcast.7, bf16[2,2,1024,512]{3,2,1,0:T(8,128)(2,1)} %w1h.1, ...), custom_call_target="tpu_custom_call" | custom-call | tf_op jit(solution)/shard_map/moe_layers/pallas_call | solution.py:447
  310.7 2.3 copy.8

commit v5 on v4

--- a/solution.py
+++ b/solution.py
@@ -176,8 +176,8 @@
             add(s, base1(2, k), 2 * ROW1, ra[s, pl.ds((4 * k + 2) * ROW1, 2 * ROW1)])
             rs(s, k, 2).start()
 
-    def r2(s):
-        for k in range(N1):
+    def r2(s, ks=range(N1)):
+        for k in ks:
             rs(s, k, 1).wait_recv()
             add(s, base1(0, k), 2 * ROW1, ra[s, pl.ds(4 * k * ROW1, 2 * ROW1)])
             rs(s, k, 3).start()
@@ -188,8 +188,8 @@
             add(s, base1(2, k), ROW1, rb[s, pl.ds((2 * k + 1) * ROW1, ROW1)])
             rs(s, k, 4).start()
 
-    def r45(s):
-        for k in range(N1):
+    def r45(s, ks=range(N1)):
+        for k in ks:
             rs(s, k, 3).wait_recv()
             rs(s, k, 4).wait_recv()
             rows = pl.ds(base1(0, k), ROW1)
@@ -344,7 +344,7 @@
     r1(1)
     feed(2)
     g1(0)
-    start([rs(1, k, 1) for k in range(N1)])
+    start([rs(1, k, 1) for k in (2, 3, 0, 1)])
     clear(0)
     r3(1)
     feed(2)
@@ -367,10 +367,10 @@
 
     plan2 = {
         2: [load(1, 0)],
-        4: [lambda: wait_recv(w_forward(0)), load(1, 2)],
-        8: [loaded(1, 0), lambda: r2(1), lambda: feed(24)],
+        4: [lambda: wait_recv(w_forward(0)), load(1, 2), lambda: r2(1, (2, 3))],
+        8: [loaded(1, 0), lambda: r2(1, (0, 1)), lambda: feed(24)],
         10: [loaded(1, 2)],
-        11: [lambda: r45(1)],
+        11: [lambda: r45(1, (2, 3, 0, 1))],
     }
 
     def second_a(m, _):

time: 313 us -> 314 us (level)
  no operation moved by 1% of the time
where the time goes in v5:
time: 314 us; the launch traced here: 313 us
  Pallas kernels  311 us (99%)
    pallas_call x1, Pallas kernels, device_body(): pl.pallas_call(moe_kernel, name='moe_layers', out_shape=[jax.ShapeDtypeSt...  311 us

profile of v5, /device:TPU:0, one launch (start us, length us, event | category | flops | bytes accessed | tf_op | source)
XLA Modules:
  0.0 313.4 jit_solution(231363839871223411)
XLA Ops:
  0.0 311.1 %moe_layers.1 = (bf16[2,256,1024]{2,1,0:T(8,128)(2,1)}, bf16[6,1024,512]{2,1,0:T(8,128)(2,1)}, bf16[6,1024,512]{2,1,0:T(8,128)(2,1)}, bf16[6,512,1024]{2,1,0:T(8,128)(2,1)}) custom-call(bf16[2,256,1024]{2,1,0:T(8,128)(2,1)} %tok.1, s32[32,256]{1,0:T(8,128)} %bitcast.6, f32[32,256]{1,0:T(8,128)} %bitcast.7, bf16[2,2,1024,512]{3,2,1,0:T(8,128)(2,1)} %w1h.1, ...), custom_call_target="tpu_custom_call" | custom-call | tf_op jit(solution)/shard_map/moe_layers/pallas_call | solution.py:447
  311.1 2.3 copy.8
